TPU v7x, 32 devices: a whole 2x2x4 slice. The times are simulated.
32 devices in a mesh: gx: 8 (over z, y), gy: 4 (over x, core).
Axes of the slice: x: 2, y: 2, z: 4, core: 2. Of those that a mesh axis runs over, the one named last changes fastest.
Arguments:
- disp_now: float32 [3, 8, 128, 512], P(None, None, 'gx', 'gy'), may hold values from -6 to 6
- disp_prev: float32 [3, 8, 128, 512], P(None, None, 'gx', 'gy'), may hold values from -6 to 6
- density: float32 [8, 128, 512], P(None, 'gx', 'gy'), may hold values from 1 to 2
- moduli: float32 [2, 8, 128, 512], P(None, None, 'gx', 'gy'), may hold values from 0.3 to 1
- coarse: float32 [64, 24, 256], P(('gx', 'gy')), may hold values from -6 to 6
- block_route: int32 [64], replicated, may hold values from 0 to 127, as said below
- ranges: int32 [8, 4, 2], P('gx', 'gy'), may hold values from 1 to 8, as said below
- offsets: int32 [8, 4, 4, 3], P('gx', 'gy'), may hold values from 0 to 24, as said below
Outputs:
- incident: float32 [2, 3, 8, 128, 512], P(None, None, None, 'gx', 'gy')
- disp_mid: float32 [3, 8, 128, 512], P(None, None, 'gx', 'gy')
- disp_next: float32 [3, 8, 128, 512], P(None, None, 'gx', 'gy')
Inputs may be any that keep to these rules, and one draw needn't show every extreme that they name: block_route[b] = tile 4 + g with tile = X 4 + Y; no slot is named twice; the slots named of a tile are g = 0 to k - 1 for its count k, which is 1 on half of the tiles, 2 on a quarter and 4 on a quarter. ranges[X, Y] = (lo, hi) with hi = 2 k for the tile's count k in block_route, and 1 <= lo < hi. offsets[X, Y, g] = (oz, oe, on) in fine cells with oz at most 5.
All inputs are finite; a program needn't handle non-finite values.
Results may differ from a plain program's by a relative error of at most 0.000073.
Values sent between devices are 32-bit elements; how exact they have to be, the bound alone decides.
No kernel may reach another device: no remote copies, remote signals or barrier semaphores. Data moves between devices by JAX's collectives and lax.ppermute only.
A program may use at most 64 MiB of HBM per device.

v0:
```python
import jax
import jax.numpy as jnp
from jax import lax
from jax.sharding import PartitionSpec as P

step_square = 0.05
time_weights = ((-0.0595, 0.7735, 0.3315, -0.0455), (-0.063756, 0.607068, 0.517132, -0.060444))


def padded_2(cells, sides, width):
    for axis, dim in sides:
        count = lax.axis_size(axis)
        ends = count - 1
        head = lax.slice_in_dim(cells, 0, width, axis=dim)
        tail = lax.slice_in_dim(cells, cells.shape[dim] - width, cells.shape[dim], axis=dim)
        cells = jnp.concatenate(
            [
                lax.ppermute(tail, axis, [(i, (i + 1) % count) for i in range(ends)]),
                cells,
                lax.ppermute(head, axis, [((i + 1) % count, i) for i in range(ends)]),
            ],
            axis=dim,
        )
    return cells


def trimmed(values_in, axis_pos, head_cut, tail_cut):
    axis_pos = axis_pos % values_in.ndim
    return lax.slice_in_dim(
        values_in, head_cut, values_in.shape[axis_pos] - tail_cut, axis=axis_pos
    )


def inner_cut(values_in, axes_list):
    for axis_pos in axes_list:
        values_in = trimmed(values_in, axis_pos, 1, 1)
    return values_in


def operate(motion, shear_mod, lame_mod):
    spatial = (-3, -2, -1)
    stiffness = lame_mod + 2.0 * shear_mod
    components = []
    for i in range(3):
        component = motion[..., i, :, :, :]
        total = None
        for j in range(3):
            axis_along = spatial[j]
            others = tuple((a for a in spatial if a != axis_along))
            modulus = stiffness if j == i else shear_mod
            values = inner_cut(component, others)
            weights = inner_cut(modulus, others)
            middle = trimmed(values, axis_along, 1, 1)
            forward = trimmed(values, axis_along, 2, 0)
            backward = trimmed(values, axis_along, 0, 2)
            modulus_mid = trimmed(weights, axis_along, 1, 1)
            modulus_next = trimmed(weights, axis_along, 2, 0)
            modulus_prior = trimmed(weights, axis_along, 0, 2)
            flux_term = 0.5 * (modulus_mid + modulus_next) * (forward - middle) - 0.5 * (
                modulus_mid + modulus_prior
            ) * (middle - backward)
            total = flux_term if total is None else total + flux_term
        for j in range(3):
            if j != i:
                across = spatial[i]
                axis_along = spatial[j]
                third_axis = [a for a in spatial if a != across and a != axis_along][0]
                partner = motion[..., j, :, :, :]
                gradient = 0.5 * (
                    trimmed(partner, axis_along, 2, 0) - trimmed(partner, axis_along, 0, 2)
                )
                flux_term = trimmed(lame_mod, axis_along, 1, 1) * gradient
                total = total + trimmed(
                    0.5 * (trimmed(flux_term, across, 2, 0) - trimmed(flux_term, across, 0, 2)),
                    third_axis,
                    1,
                    1,
                )
                gradient = 0.5 * (trimmed(partner, across, 2, 0) - trimmed(partner, across, 0, 2))
                flux_term = trimmed(shear_mod, across, 1, 1) * gradient
                total = total + trimmed(
                    0.5
                    * (trimmed(flux_term, axis_along, 2, 0) - trimmed(flux_term, axis_along, 0, 2)),
                    third_axis,
                    1,
                    1,
                )
        components.append(total)
    return jnp.stack(components, axis=-4)


def hat_matrix(offset_cells, fine_count, coarse_count):
    fine_pos = (offset_cells[:, None] + jnp.arange(fine_count, dtype=jnp.int32)[None, :]) * 4
    base_index = fine_pos // 25
    fraction = (fine_pos % 25).astype(jnp.float32) / 25.0
    column = jnp.arange(coarse_count, dtype=jnp.int32)
    first = jnp.where(
        column[None, None, :] == base_index[:, :, None], 1.0 - fraction[:, :, None], 0.0
    )
    second = jnp.where(
        column[None, None, :] == base_index[:, :, None] + 1, fraction[:, :, None], 0.0
    )
    return first + second


def spread(samples, offset_cells, east_cells, north_cells):
    level_pos = (offset_cells[:, 0:1] + jnp.arange(2, dtype=jnp.int32)[None, :]).astype(
        jnp.float32
    ) * (4.0 / 25.0)
    upper_level = samples[:, :, :, 0][:, :, :, None]
    lower_level = samples[:, :, :, 1][:, :, :, None]
    vertical = (
        upper_level * (1.0 - level_pos)[:, None, None, :, None, None]
        + lower_level * level_pos[:, None, None, :, None, None]
    )
    east_matrix = hat_matrix(offset_cells[:, 1], east_cells, samples.shape[-2])
    north_matrix = hat_matrix(offset_cells[:, 2], north_cells, samples.shape[-1])
    eastern = jnp.einsum(
        "kxa,kncjay->kncjxy", east_matrix, vertical, precision=lax.Precision.HIGHEST
    )
    return jnp.einsum("kncjxa,kya->kncjxy", eastern, north_matrix, precision=lax.Precision.HIGHEST)


def level_pad(values_in):
    return jnp.pad(values_in, [(0, 0)] * (values_in.ndim - 3) + [(1, 1), (0, 0), (0, 0)])


def local(disp_now, disp_prev, density, moduli, coarse, block_route, ranges, offsets):
    levels = disp_now.shape[1]
    groups = levels // 2
    east_cells = disp_now.shape[2]
    north_cells = disp_now.shape[3]
    coarse_east = (east_cells + 23) * 4 // 25 + 2
    coarse_north = (north_cells + 23) * 4 // 25 + 2
    point_total = coarse_east * coarse_north
    block_hold = coarse.shape[0]
    samples_in = coarse.shape[1] // 6
    east_count = lax.axis_size("gx")
    north_count = lax.axis_size("gy")
    device_count = east_count * north_count
    own_east = lax.axis_index("gx")
    own_north = lax.axis_index("gy")
    own_flat = own_east * north_count + own_north
    start_pad = level_pad(
        padded_2(jnp.concatenate([moduli, disp_now], axis=0), (("gx", 2), ("gy", 3)), 1)
    )
    shear_mod = start_pad[0]
    lame_mod = start_pad[1]
    now_pad = start_pad[2:5]

    def advance(padded, current, previous, forcing):
        return (
            2.0 * current
            - previous
            + step_square / density * (operate(padded, shear_mod, lame_mod) + forcing)
        )

    weights = jnp.array(time_weights, jnp.float32)
    count_here = coarse.shape[0]
    width_here = coarse.shape[2]
    blended = jnp.einsum(
        "nt,ktpq->knpq",
        weights,
        coarse.reshape(count_here, samples_in, 6, width_here),
        precision=lax.Precision.HIGHEST,
    )
    payload = blended.reshape(count_here, 12, width_here)
    row_width = payload.shape[1]
    piece_width = payload.shape[2]
    group_ids = jnp.arange(groups, dtype=jnp.int32)
    local_tiles = lax.dynamic_slice_in_dim(block_route, own_flat * block_hold, block_hold) // groups
    targets = jnp.arange(device_count, dtype=jnp.int32)
    sending = (local_tiles[None, :] == targets[:, None]).astype(jnp.float32)
    outgoing = sending[:, :, None, None] * payload[None]
    received = lax.all_to_all(
        outgoing, ("gx", "gy"), split_axis=0, concat_axis=0, tiled=True
    ).reshape(device_count * block_hold, row_width, piece_width)
    select = (block_route[None, :] == own_flat * groups + group_ids[:, None]).astype(jnp.float32)
    arrived = jnp.einsum("gk,kpq->gpq", select, received, precision=lax.Precision.HIGHEST)
    slot_data = arrived[:, :, :point_total]
    samples = slot_data.reshape(groups, 2, 3, 2, coarse_east, coarse_north)
    fine_values = spread(samples, offsets[0, 0], east_cells, north_cells)
    incident = fine_values.transpose(1, 2, 0, 3, 4, 5).reshape(
        2, 3, levels, east_cells, north_cells
    )
    low_level = ranges[0, 0, 0]
    high_level = ranges[0, 0, 1]
    level_ids = jnp.arange(levels, dtype=jnp.int32)[:, None, None]
    outer_mask = (level_ids < low_level).astype(jnp.float32)
    inner_mask = ((level_ids >= low_level) & (level_ids < high_level)).astype(jnp.float32)
    masked = jnp.stack(
        [
            outer_mask * incident[0],
            inner_mask * incident[0],
            outer_mask * incident[1],
            inner_mask * incident[1],
        ]
    )
    padded_parts = level_pad(padded_2(masked, (("gx", 3), ("gy", 4)), 1))
    applied = operate(padded_parts, shear_mod, lame_mod)
    force_first = inner_mask * applied[0] - outer_mask * applied[1]
    force_second = inner_mask * applied[2] - outer_mask * applied[3]
    disp_mid = advance(now_pad, disp_now, disp_prev, force_first)
    mid_pad = level_pad(padded_2(disp_mid, (("gx", 2), ("gy", 3)), 1))
    disp_next = advance(mid_pad, disp_mid, disp_now, force_second)
    return (incident, disp_mid, disp_next)


def solution(mesh):
    return jax.shard_map(
        local,
        mesh=mesh,
        in_specs=(
            P(None, None, "gx", "gy"),
            P(None, None, "gx", "gy"),
            P(None, "gx", "gy"),
            P(None, None, "gx", "gy"),
            P(("gx", "gy"), None, None),
            P(),
            P("gx", "gy", None),
            P("gx", "gy", None, None),
        ),
        out_specs=(
            P(None, None, None, "gx", "gy"),
            P(None, None, "gx", "gy"),
            P(None, None, "gx", "gy"),
        ),
        check_vma=False,
    )
```

profile of v0, /device:TPU:5, one launch (start us, length us, event | category | flops | bytes accessed | tf_op | source)
XLA Modules:
  0.0 120.1 jit_solution(8556462186664424248)
XLA Ops:
  0.6 0.7 and_select_fusion
  1.4 0.8 copy.32
  2.2 0.9 convolution_bitcast_fusion.2
  3.2 1.2 broadcast_multiply_fusion
  4.4 6.4 %all-to-all-start = ((f32[32,2,12,256]{3,1,2,0:T(2,128)}), f32[32,2,12,256]{3,1,2,0:T(2,128)S(1)}, u32[]{:S(2)}, u32[]{:S(2)}) async-start(f32[32,2,12,256]{3,1,2,0:T(2,128)} %broadcast_multiply_fusion), calls=%async_computation | async-start | bytes 1572864 | tf_op jit(solution)/shard_map/all_to_all | solution.py:175
  10.8 3.1 %collective-permute-start = (f32[5,8,1,128]{3,2,1,0:T(1,128)S(1)}, f32[5,8,1,128]{3,2,1,0:T(1,128)S(1)}, u32[]{:S(2)}, u32[]{:S(2)}) collective-permute-start(f32[5,8,1,128]{3,2,1,0:T(1,128)S(1)} %get-tuple-element.79), channel_id=1, source_target_pairs={{0,4},{4,8},{8,12},{12,16},{16,20},{20,24},{24,28},{1,5},{5,9},{9,... | collective-permute-start | bytes 61448 | tf_op jit(solution)/shard_map/ppermute | solution.py:18
  13.9 2.2 %collective-permute-start.1 = (f32[5,8,1,128]{3,2,1,0:T(1,128)S(1)}, f32[5,8,1,128]{3,2,1,0:T(1,128)S(1)}, u32[]{:S(2)}, u32[]{:S(2)}) collective-permute-start(f32[5,8,1,128]{3,2,1,0:T(1,128)S(1)} %get-tuple-element.80), channel_id=1, source_target_pairs={{4,0},{8,4},{12,8},{16,12},{20,16},{24,20},{28,24},{5,1},{9,5},{13... | collective-permute-start | bytes 61448 | tf_op jit(solution)/shard_map/ppermute | solution.py:20
  16.9 0.6 fusion.375
  17.5 0.6 broadcast_divide_fusion
  18.1 1.3 %compare_convert_fusion = (f32[8]{0:T(128)S(1)}, f32[8]{0:T(128)S(1)}) fusion(s32[]{:T(128)} %bitcast.31, s32[]{:T(128)} %bitcast.32), kind=kLoop, calls=%fused_computation.521 | loop fusion | flops 48 | bytes 72 | tf_op jit(solution)/shard_map/convert_element_type | solution.py:189
  19.4 4.4 %collective-permute-done = f32[5,8,1,128]{3,2,1,0:T(1,128)S(1)} collective-permute-done((f32[5,8,1,128]{3,2,1,0:T(1,128)S(1)}, f32[5,8,1,128]{3,2,1,0:T(1,128)S(1)}, u32[]{:S(2)}, u32[]{:S(2)}) %collective-permute-start) | collective-permute-done | bytes 20512 | tf_op jit(solution)/shard_map/ppermute | solution.py:18
  24.1 3.9 %collective-permute-start.2 = (f32[5,8,18,1]{3,2,1,0:T(8,128)S(1)}, f32[5,8,18,1]{3,2,1,0:T(8,128)S(1)}, u32[]{:S(2)}, u32[]{:S(2)}) collective-permute-start(f32[5,8,18,1]{3,2,1,0:T(8,128)S(1)} %get-tuple-element.75), channel_id=1, source_target_pairs={{0,1},{1,2},{2,3},{4,5},{5,6},{6,7},{8,9},{9,10},{10,11},{12,13},{... | collective-permute-start | bytes 8648 | tf_op jit(solution)/shard_map/ppermute | solution.py:18
  28.1 1.9 %collective-permute-start.3 = (f32[5,8,18,1]{3,2,1,0:T(8,128)S(1)}, f32[5,8,18,1]{3,2,1,0:T(8,128)S(1)}, u32[]{:S(2)}, u32[]{:S(2)}) collective-permute-start(f32[5,8,18,1]{3,2,1,0:T(8,128)S(1)} %get-tuple-element.76), channel_id=1, source_target_pairs={{1,0},{2,1},{3,2},{5,4},{6,5},{7,6},{9,8},{10,9},{11,10},{13,12},{... | collective-permute-start | bytes 8648 | tf_op jit(solution)/shard_map/ppermute | solution.py:20
  30.0 3.8 %collective-permute-done.2 = f32[5,8,18,1]{3,2,1,0:T(8,128)S(1)} collective-permute-done((f32[5,8,18,1]{3,2,1,0:T(8,128)S(1)}, f32[5,8,18,1]{3,2,1,0:T(8,128)S(1)}, u32[]{:S(2)}, u32[]{:S(2)}) %collective-permute-start.2) | collective-permute-done | bytes 2912 | tf_op jit(solution)/shard_map/ppermute | solution.py:18
  33.8 4.4 %collective-permute-done.3 = f32[5,8,18,1]{3,2,1,0:T(8,128)S(1)} collective-permute-done((f32[5,8,18,1]{3,2,1,0:T(8,128)S(1)}, f32[5,8,18,1]{3,2,1,0:T(8,128)S(1)}, u32[]{:S(2)}, u32[]{:S(2)}) %collective-permute-start.3) | collective-permute-done | bytes 2912 | tf_op jit(solution)/shard_map/ppermute | solution.py:20
  38.2 0.6 pad_maximum_fusion.2
  38.8 0.8 broadcast_multiply_fusion.1
  39.7 1.0 fusion.142
  40.7 0.8 fusion.132
  41.5 0.8 slice_bitcast_fusion.8
  42.6 0.7 fusion.366
  43.3 0.7 fusion.373
  44.0 0.7 fusion.358
  44.9 1.1 fusion.257
  46.0 0.6 copy-done.18
  46.7 1.1 fusion.233
  48.1 0.5 reshape.417
  49.2 0.6 convolution_bitcast_fusion.1
  50.5 0.5 copy-done.4
  51.1 5.1 %collective-permute-start.4 = (f32[4,3,8,1,128]{4,3,2,1,0:T(1,128)S(1)}, f32[4,3,8,1,128]{4,3,2,1,0:T(1,128)S(1)}, u32[]{:S(2)}, u32[]{:S(2)}) collective-permute-start(f32[4,3,8,1,128]{4,3,2,1,0:T(1,128)S(1)} %get-tuple-element.50), channel_id=1, source_target_pairs={{0,4},{4,8},{8,12},{12,16},{16,20},{20,24},{24,28},{1,5},{5,9},{9,... | collective-permute-start | bytes 147464 | tf_op jit(solution)/shard_map/ppermute | solution.py:18
  56.2 1.9 %collective-permute-start.5 = (f32[4,3,8,1,128]{4,3,2,1,0:T(1,128)S(1)}, f32[4,3,8,1,128]{4,3,2,1,0:T(1,128)S(1)}, u32[]{:S(2)}, u32[]{:S(2)}) collective-permute-start(f32[4,3,8,1,128]{4,3,2,1,0:T(1,128)S(1)} %get-tuple-element.51), channel_id=1, source_target_pairs={{4,0},{8,4},{12,8},{16,12},{20,16},{24,20},{28,24},{5,1},{9,5},{13... | collective-permute-start | bytes 147464 | tf_op jit(solution)/shard_map/ppermute | solution.py:20
  58.1 0.7 fusion.374
  58.8 6.1 %collective-permute-done.5 = f32[4,3,8,1,128]{4,3,2,1,0:T(1,128)S(1)} collective-permute-done((f32[4,3,8,1,128]{4,3,2,1,0:T(1,128)S(1)}, f32[4,3,8,1,128]{4,3,2,1,0:T(1,128)S(1)}, u32[]{:S(2)}, u32[]{:S(2)}) %collective-permute-start.5) | collective-permute-done | bytes 49184 | tf_op jit(solution)/shard_map/ppermute | solution.py:20
  64.9 0.6 copy-done.48
  66.1 1.3 %copy.42 = f32[4,3,8,18,1]{3,2,4,1,0:T(8,128)} copy(f32[4,3,8,18,1]{4,3,2,1,0:T(8,128)S(1)} %get-tuple-element.26) | data formatting | bytes 13824 | tf_op jit(solution)/shard_map/slice | solution.py:15
  67.5 3.0 %collective-permute-start.6 = (f32[4,3,8,18,1]{3,2,4,1,0:T(8,128)}, f32[4,3,8,18,1]{3,2,4,1,0:T(8,128)}, u32[]{:S(2)}, u32[]{:S(2)}) collective-permute-start(f32[4,3,8,18,1]{3,2,4,1,0:T(8,128)} %copy.42), channel_id=1, source_target_pairs={{0,1},{1,2},{2,3},{4,5},{5,6},{6,7},{8,9},{9,10},{10,11},{12,13},{... | collective-permute-start | bytes 20744 | tf_op jit(solution)/shard_map/ppermute | solution.py:18
  70.5 1.3 %copy.43 = f32[4,3,8,18,1]{3,2,4,1,0:T(8,128)} copy(f32[4,3,8,18,1]{4,3,2,1,0:T(8,128)S(1)} %get-tuple-element.27) | data formatting | bytes 13824 | tf_op jit(solution)/shard_map/slice | solution.py:14
  71.8 2.2 %collective-permute-start.7 = (f32[4,3,8,18,1]{3,2,4,1,0:T(8,128)}, f32[4,3,8,18,1]{3,2,4,1,0:T(8,128)}, u32[]{:S(2)}, u32[]{:S(2)}) collective-permute-start(f32[4,3,8,18,1]{3,2,4,1,0:T(8,128)} %copy.43), channel_id=1, source_target_pairs={{1,0},{2,1},{3,2},{5,4},{6,5},{7,6},{9,8},{10,9},{11,10},{13,12},{... | collective-permute-start | bytes 20744 | tf_op jit(solution)/shard_map/ppermute | solution.py:20
  74.1 2.0 %fusion.211 = (f32[1,8,16,128]{3,2,1,0:T(8,128)}, f32[8,16,128]{2,1,0:T(8,128)}, f32[8,16,128]{2,1,0:T(8,128)}) fusion(f32[10,16,128]{2,1,0:T(8,128)} %get-tuple-element.156, f32[10,16,128]{2,1,0:T(8,128)} %get-tuple-element.155, f32[10,16,128]{2,1,0:T(8,128)} %get-tuple-element.140, f32[10,16,128]{2,1,0:T(8,128)} %get-tuple-element.139, ...), kind=kLoop, calls=%fused_computation.351 | loop fusion | flops 540672 | bytes 1703936 | tf_op jit(solution)/shard_map/stack | solution.py:89
  76.1 1.5 %copy.44 = f32[4,3,8,18,1]{4,3,2,1,0:T(8,128)S(1)} copy(f32[4,3,8,18,1]{3,2,4,1,0:T(8,128)} %collective-permute-done.6) | data formatting | bytes 13824 | tf_op jit(solution)/shard_map/ppermute | solution.py:18
  77.6 1.5 %copy.45 = f32[4,3,8,18,1]{4,3,2,1,0:T(8,128)S(1)} copy(f32[4,3,8,18,1]{3,2,4,1,0:T(8,128)} %collective-permute-done.7) | data formatting | bytes 13824 | tf_op jit(solution)/shard_map/ppermute | solution.py:20
  79.1 2.5 %pad_maximum_fusion = f32[4,3,8,18,130]{4,3,2,1,0:T(8,128)S(1)} fusion(f32[4,3,8,18,1]{4,3,2,1,0:T(8,128)S(1)} %copy.45, f32[4,3,8,1,128]{4,3,2,1,0:T(1,128)} %copy-done.48, f32[1,3,8,16,128]{4,3,2,1,0:T(8,128)} %copy-done.7, f32[1,3,8,16,128]{4,3,2,1,0:T(8,128)S(1)} %get-tuple-element.119, f32[1,3,8,16,128]{4,3,2,1,0:T(8,128)} %copy-done.8, ...), kind=kLoop, calls=%fused_computation.3 | loop fusion | flops 1572480 | bytes 1797120 | tf_op jit(solution)/shard_map/concatenate | solution.py:16
  81.9 0.6 copy-done.41
  82.8 0.8 copy-done.30
  84.0 0.7 copy-done.32
  85.2 0.6 copy-done.29
  86.3 0.7 copy-done.31
  87.6 0.6 copy-done.40
  88.7 0.7 copy-done.15
  89.5 0.8 fusion.56
  90.4 0.8 fusion.36
  91.3 0.6 fusion.16
  92.0 0.8 copy-done.27
  93.2 3.6 %collective-permute-start.8 = (f32[3,8,1,128]{3,2,1,0:T(1,128)S(1)}, f32[3,8,1,128]{3,2,1,0:T(1,128)S(1)}, u32[]{:S(2)}, u32[]{:S(2)}) collective-permute-start(f32[3,8,1,128]{3,2,1,0:T(1,128)S(1)} %get-tuple-element.105), channel_id=1, source_target_pairs={{0,4},{4,8},{8,12},{12,16},{16,20},{20,24},{24,28},{1,5},{5,9},{9,... | collective-permute-start | bytes 36872 | tf_op jit(solution)/shard_map/ppermute | solution.py:18
  96.8 1.9 %collective-permute-start.9 = (f32[3,8,1,128]{3,2,1,0:T(1,128)S(1)}, f32[3,8,1,128]{3,2,1,0:T(1,128)S(1)}, u32[]{:S(2)}, u32[]{:S(2)}) collective-permute-start(f32[3,8,1,128]{3,2,1,0:T(1,128)S(1)} %get-tuple-element.106), channel_id=1, source_target_pairs={{4,0},{8,4},{12,8},{16,12},{20,16},{24,20},{28,24},{5,1},{9,5},{13... | collective-permute-start | bytes 36872 | tf_op jit(solution)/shard_map/ppermute | solution.py:20
  98.7 3.6 %collective-permute-done.9 = f32[3,8,1,128]{3,2,1,0:T(1,128)S(1)} collective-permute-done((f32[3,8,1,128]{3,2,1,0:T(1,128)S(1)}, f32[3,8,1,128]{3,2,1,0:T(1,128)S(1)}, u32[]{:S(2)}, u32[]{:S(2)}) %collective-permute-start.9) | collective-permute-done | bytes 12320 | tf_op jit(solution)/shard_map/ppermute | solution.py:20
  102.6 4.8 %collective-permute-start.10 = (f32[3,8,18,1]{3,2,1,0:T(8,128)S(1)}, f32[3,8,18,1]{3,2,1,0:T(8,128)S(1)}, u32[]{:S(2)}, u32[]{:S(2)}) collective-permute-start(f32[3,8,18,1]{3,2,1,0:T(8,128)S(1)} %get-tuple-element.81), channel_id=1, source_target_pairs={{0,1},{1,2},{2,3},{4,5},{5,6},{6,7},{8,9},{9,10},{10,11},{12,13},{... | collective-permute-start | bytes 5192 | tf_op jit(solution)/shard_map/ppermute | solution.py:18
  107.3 1.9 %collective-permute-start.11 = (f32[3,8,18,1]{3,2,1,0:T(8,128)S(1)}, f32[3,8,18,1]{3,2,1,0:T(8,128)S(1)}, u32[]{:S(2)}, u32[]{:S(2)}) collective-permute-start(f32[3,8,18,1]{3,2,1,0:T(8,128)S(1)} %get-tuple-element.82), channel_id=1, source_target_pairs={{1,0},{2,1},{3,2},{5,4},{6,5},{7,6},{9,8},{10,9},{11,10},{13,12},{... | collective-permute-start | bytes 5192 | tf_op jit(solution)/shard_map/ppermute | solution.py:20
  109.3 0.8 copy.39
  110.1 0.9 collective-permute-done.10
  111.0 4.4 %collective-permute-done.11 = f32[3,8,18,1]{3,2,1,0:T(8,128)S(1)} collective-permute-done((f32[3,8,18,1]{3,2,1,0:T(8,128)S(1)}, f32[3,8,18,1]{3,2,1,0:T(8,128)S(1)}, u32[]{:S(2)}, u32[]{:S(2)}) %collective-permute-start.11) | collective-permute-done | bytes 1760 | tf_op jit(solution)/shard_map/ppermute | solution.py:20
  116.0 0.9 copy-done.13
  117.3 0.7 copy-done.1
  119.3 0.8 fusion.110
  (187 shorter events, 9.9 us)
Async XLA Ops:
  3.1 7.6 %copy-start.50 = (f32[2,8,16,128]{3,2,1,0:T(8,128)S(1)}, f32[2,8,16,128]{3,2,1,0:T(8,128)}, u32[]{:S(2)}) copy-start(f32[2,8,16,128]{3,2,1,0:T(8,128)} %param.12) | copy-start | bytes 393220
  3.2 7.6 %copy-start.26 = (f32[3,8,16,128]{3,2,1,0:T(8,128)S(1)}, f32[3,8,16,128]{3,2,1,0:T(8,128)}, u32[]{:S(2)}) copy-start(f32[3,8,16,128]{3,2,1,0:T(8,128)} %param.9) | copy-start | bytes 589828
  4.3 11.8 %copy-start.53 = (s32[1,1,4,3]{2,1,3,0:T(1,128)S(1)}, s32[1,1,4,3]{2,1,3,0:T(1,128)}, u32[]{:S(2)}) copy-start(s32[1,1,4,3]{2,1,3,0:T(1,128)} %param.16) | copy-start | bytes 148
  4.3 12.5 %copy-start.52 = (s32[1,1,2]{2,1,0:T(1,128)S(1)}, s32[1,1,2]{2,1,0:T(1,128)}, u32[]{:S(2)}) copy-start(s32[1,1,2]{2,1,0:T(1,128)} %param.15) | copy-start | bytes 28
  4.3 13.1 %copy-start.51 = (f32[8,16,128]{2,1,0:T(8,128)S(1)}, f32[8,16,128]{2,1,0:T(8,128)}, u32[]{:S(2)}) copy-start(f32[8,16,128]{2,1,0:T(8,128)} %param.11) | copy-start | bytes 196612
  4.4 43.4 %all-to-all-start = ((f32[32,2,12,256]{3,1,2,0:T(2,128)}), f32[32,2,12,256]{3,1,2,0:T(2,128)S(1)}, u32[]{:S(2)}, u32[]{:S(2)}) async-start(f32[32,2,12,256]{3,1,2,0:T(2,128)} %broadcast_multiply_fusion), calls=%async_computation | async-start | bytes 1572864 | tf_op jit(solution)/shard_map/all_to_all | solution.py:175
  10.8 13.0 %collective-permute-start = (f32[5,8,1,128]{3,2,1,0:T(1,128)S(1)}, f32[5,8,1,128]{3,2,1,0:T(1,128)S(1)}, u32[]{:S(2)}, u32[]{:S(2)}) collective-permute-start(f32[5,8,1,128]{3,2,1,0:T(1,128)S(1)} %get-tuple-element.79), channel_id=1, source_target_pairs={{0,4},{4,8},{8,12},{12,16},{16,20},{20,24},{24,28},{1,5},{5,9},{9,... | collective-permute-start | bytes 61448 | tf_op jit(solution)/shard_map/ppermute | solution.py:18
  13.9 9.9 %collective-permute-start.1 = (f32[5,8,1,128]{3,2,1,0:T(1,128)S(1)}, f32[5,8,1,128]{3,2,1,0:T(1,128)S(1)}, u32[]{:S(2)}, u32[]{:S(2)}) collective-permute-start(f32[5,8,1,128]{3,2,1,0:T(1,128)S(1)} %get-tuple-element.80), channel_id=1, source_target_pairs={{4,0},{8,4},{12,8},{16,12},{20,16},{24,20},{28,24},{5,1},{9,5},{13... | collective-permute-start | bytes 61448 | tf_op jit(solution)/shard_map/ppermute | solution.py:20
  24.1 9.7 %collective-permute-start.2 = (f32[5,8,18,1]{3,2,1,0:T(8,128)S(1)}, f32[5,8,18,1]{3,2,1,0:T(8,128)S(1)}, u32[]{:S(2)}, u32[]{:S(2)}) collective-permute-start(f32[5,8,18,1]{3,2,1,0:T(8,128)S(1)} %get-tuple-element.75), channel_id=1, source_target_pairs={{0,1},{1,2},{2,3},{4,5},{5,6},{6,7},{8,9},{9,10},{10,11},{12,13},{... | collective-permute-start | bytes 8648 | tf_op jit(solution)/shard_map/ppermute | solution.py:18
  28.1 10.1 %collective-permute-start.3 = (f32[5,8,18,1]{3,2,1,0:T(8,128)S(1)}, f32[5,8,18,1]{3,2,1,0:T(8,128)S(1)}, u32[]{:S(2)}, u32[]{:S(2)}) collective-permute-start(f32[5,8,18,1]{3,2,1,0:T(8,128)S(1)} %get-tuple-element.76), channel_id=1, source_target_pairs={{1,0},{2,1},{3,2},{5,4},{6,5},{7,6},{9,8},{10,9},{11,10},{13,12},{... | collective-permute-start | bytes 8648 | tf_op jit(solution)/shard_map/ppermute | solution.py:20
  39.7 1.9 %copy-start.2 = (f32[10,18,130]{2,1,0:T(8,128)}, f32[10,18,130]{2,1,0:T(8,128)S(1)}, u32[]{:S(2)}) copy-start(f32[10,18,130]{2,1,0:T(8,128)S(1)} %get-tuple-element.37) | copy-start | bytes 280804
  39.7 1.9 %copy-start.12 = (f32[10,18,130]{2,1,0:T(8,128)}, f32[10,18,130]{2,1,0:T(8,128)S(1)}, u32[]{:S(2)}) copy-start(f32[10,18,130]{2,1,0:T(8,128)S(1)} %get-tuple-element.41) | copy-start | bytes 280804
  39.7 6.3 %copy-start = (f32[10,18,130]{2,1,0:T(8,128)}, f32[10,18,130]{2,1,0:T(8,128)S(1)}, u32[]{:S(2)}) copy-start(f32[10,18,130]{2,1,0:T(8,128)S(1)} %get-tuple-element.38) | copy-start | bytes 280804
  44.8 1.2 %copy-start.10 = (f32[10,18,130]{2,1,0:T(8,128)}, f32[10,18,130]{2,1,0:T(8,128)S(1)}, u32[]{:S(2)}) copy-start(f32[10,18,130]{2,1,0:T(8,128)S(1)} %multiply_add_fusion) | copy-start | bytes 280804
  47.7 0.9 copy-start.54
  51.0 13.9 %copy-start.7 = (f32[1,3,8,16,128]{4,3,2,1,0:T(8,128)}, f32[1,3,8,16,128]{4,3,2,1,0:T(8,128)S(1)}, u32[]{:S(2)}) copy-start(f32[1,3,8,16,128]{4,3,2,1,0:T(8,128)S(1)} %get-tuple-element.120) | copy-start | bytes 589828
  51.0 13.9 %copy-start.8 = (f32[1,3,8,16,128]{4,3,2,1,0:T(8,128)}, f32[1,3,8,16,128]{4,3,2,1,0:T(8,128)S(1)}, u32[]{:S(2)}) copy-start(f32[1,3,8,16,128]{4,3,2,1,0:T(8,128)S(1)} %get-tuple-element.159) | copy-start | bytes 589828
  51.0 13.9 %copy-start.9 = (f32[1,3,8,16,128]{4,3,2,1,0:T(8,128)}, f32[1,3,8,16,128]{4,3,2,1,0:T(8,128)S(1)}, u32[]{:S(2)}) copy-start(f32[1,3,8,16,128]{4,3,2,1,0:T(8,128)S(1)} %get-tuple-element.160) | copy-start | bytes 589828
  51.1 7.7 %collective-permute-start.4 = (f32[4,3,8,1,128]{4,3,2,1,0:T(1,128)S(1)}, f32[4,3,8,1,128]{4,3,2,1,0:T(1,128)S(1)}, u32[]{:S(2)}, u32[]{:S(2)}) collective-permute-start(f32[4,3,8,1,128]{4,3,2,1,0:T(1,128)S(1)} %get-tuple-element.50), channel_id=1, source_target_pairs={{0,4},{4,8},{8,12},{12,16},{16,20},{20,24},{24,28},{1,5},{5,9},{9,... | collective-permute-start | bytes 147464 | tf_op jit(solution)/shard_map/ppermute | solution.py:18
  56.2 8.7 %collective-permute-start.5 = (f32[4,3,8,1,128]{4,3,2,1,0:T(1,128)S(1)}, f32[4,3,8,1,128]{4,3,2,1,0:T(1,128)S(1)}, u32[]{:S(2)}, u32[]{:S(2)}) collective-permute-start(f32[4,3,8,1,128]{4,3,2,1,0:T(1,128)S(1)} %get-tuple-element.51), channel_id=1, source_target_pairs={{4,0},{8,4},{12,8},{16,12},{20,16},{24,20},{28,24},{5,1},{9,5},{13... | collective-permute-start | bytes 147464 | tf_op jit(solution)/shard_map/ppermute | solution.py:20
  58.8 6.1 %copy-start.47 = (f32[4,3,8,1,128]{4,3,2,1,0:T(1,128)}, f32[4,3,8,1,128]{4,3,2,1,0:T(1,128)S(1)}, u32[]{:S(2)}) copy-start(f32[4,3,8,1,128]{4,3,2,1,0:T(1,128)S(1)} %collective-permute-done.4) | copy-start | bytes 147460
  67.4 6.6 %copy-start.3 = (f32[10,18,130]{2,1,0:T(8,128)S(1)}, f32[10,18,130]{2,1,0:T(8,128)}, u32[]{:S(2)}) copy-start(f32[10,18,130]{2,1,0:T(8,128)} %copy-done.2) | copy-start | bytes 280804
  67.4 6.6 %copy-start.11 = (f32[10,18,130]{2,1,0:T(8,128)S(1)}, f32[10,18,130]{2,1,0:T(8,128)}, u32[]{:S(2)}) copy-start(f32[10,18,130]{2,1,0:T(8,128)} %copy-done.10) | copy-start | bytes 280804
  67.4 6.6 %copy-start.14 = (f32[8,16,128]{2,1,0:T(8,128)S(1)}, f32[8,16,128]{2,1,0:T(8,128)}, u32[]{:S(2)}) copy-start(f32[8,16,128]{2,1,0:T(8,128)} %get-tuple-element.11) | copy-start | bytes 196612
  67.4 6.6 %copy-start.16 = (f32[8,16,128]{2,1,0:T(8,128)S(1)}, f32[8,16,128]{2,1,0:T(8,128)}, u32[]{:S(2)}) copy-start(f32[8,16,128]{2,1,0:T(8,128)} %get-tuple-element.12) | copy-start | bytes 196612
  67.4 6.6 %copy-start.22 = (f32[8,16,128]{2,1,0:T(8,128)S(1)}, f32[8,16,128]{2,1,0:T(8,128)}, u32[]{:S(2)}) copy-start(f32[8,16,128]{2,1,0:T(8,128)} %get-tuple-element.16) | copy-start | bytes 196612
  67.4 6.6 %copy-start.24 = (f32[8,16,128]{2,1,0:T(8,128)S(1)}, f32[8,16,128]{2,1,0:T(8,128)}, u32[]{:S(2)}) copy-start(f32[8,16,128]{2,1,0:T(8,128)} %get-tuple-element.17) | copy-start | bytes 196612
  67.5 6.6 %copy-start.28 = (f32[8,18,130]{2,1,0:T(8,128)S(1)}, f32[8,18,130]{2,1,0:T(8,128)}, u32[]{:S(2)}) copy-start(f32[8,18,130]{2,1,0:T(8,128)} %get-tuple-element.33) | copy-start | bytes 224644
  67.5 6.6 %copy-start.42 = (f32[8,18,128]{2,1,0:T(8,128)S(1)}, f32[8,18,128]{2,1,0:T(8,128)}, u32[]{:S(2)}) copy-start(f32[8,18,128]{2,1,0:T(8,128)} %get-tuple-element.153) | copy-start | bytes 221188
  67.5 6.6 %copy-start.43 = (f32[8,18,128]{2,1,0:T(8,128)S(1)}, f32[8,18,128]{2,1,0:T(8,128)}, u32[]{:S(2)}) copy-start(f32[8,18,128]{2,1,0:T(8,128)} %get-tuple-element.154) | copy-start | bytes 221188
  67.5 8.6 %collective-permute-start.6 = (f32[4,3,8,18,1]{3,2,4,1,0:T(8,128)}, f32[4,3,8,18,1]{3,2,4,1,0:T(8,128)}, u32[]{:S(2)}, u32[]{:S(2)}) collective-permute-start(f32[4,3,8,18,1]{3,2,4,1,0:T(8,128)} %copy.42), channel_id=1, source_target_pairs={{0,1},{1,2},{2,3},{4,5},{5,6},{6,7},{8,9},{9,10},{10,11},{12,13},{... | collective-permute-start | bytes 20744 | tf_op jit(solution)/shard_map/ppermute | solution.py:18
  71.8 5.8 %collective-permute-start.7 = (f32[4,3,8,18,1]{3,2,4,1,0:T(8,128)}, f32[4,3,8,18,1]{3,2,4,1,0:T(8,128)}, u32[]{:S(2)}, u32[]{:S(2)}) collective-permute-start(f32[4,3,8,18,1]{3,2,4,1,0:T(8,128)} %copy.43), channel_id=1, source_target_pairs={{1,0},{2,1},{3,2},{5,4},{6,5},{7,6},{9,8},{10,9},{11,10},{13,12},{... | collective-permute-start | bytes 20744 | tf_op jit(solution)/shard_map/ppermute | solution.py:20
  81.6 0.9 copy-start.41
  82.7 0.9 copy-start.30
  83.8 0.9 copy-start.32
  84.9 0.9 copy-start.29
  86.1 0.9 copy-start.31
  87.3 0.9 copy-start.40
  88.5 0.8 copy-start.15
  88.5 0.9 copy-start.17
  88.5 0.9 copy-start.19
  88.5 0.9 copy-start.21
  88.5 0.9 copy-start.33
  88.5 1.0 copy-start.34
  89.5 0.8 copy-start.23
  89.5 0.9 copy-start.25
  89.5 0.9 copy-start.37
  89.5 0.9 copy-start.38
  90.4 0.8 copy-start.35
  90.4 0.9 copy-start.36
  91.9 0.9 copy-start.27
  91.9 0.9 copy-start.39
  91.9 0.9 copy-start.44
  91.9 1.0 copy-start.45
  91.9 1.0 copy-start.46
  91.9 1.1 copy-start.49
  93.0 16.3 %copy-start.5 = (f32[2,3,4,2,16,128]{5,4,3,1,0,2:T(8,128)S(1)}, f32[2,3,4,2,16,128]{5,4,3,1,0,2:T(8,128)}, u32[]{:S(2)}) copy-start(f32[2,3,4,2,16,128]{5,4,3,1,0,2:T(8,128)} %copy-done.4) | copy-start | bytes 1179652
  93.2 26.1 %copy-start.6 = (f32[3,8,16,128]{3,2,1,0:T(8,128)}, f32[3,8,16,128]{3,2,1,0:T(8,128)S(1)}, u32[]{:S(2)}) copy-start(f32[3,8,16,128]{3,2,1,0:T(8,128)S(1)} %fusion.116) | copy-start | bytes 589828
  93.2 5.5 %collective-permute-start.8 = (f32[3,8,1,128]{3,2,1,0:T(1,128)S(1)}, f32[3,8,1,128]{3,2,1,0:T(1,128)S(1)}, u32[]{:S(2)}, u32[]{:S(2)}) collective-permute-start(f32[3,8,1,128]{3,2,1,0:T(1,128)S(1)} %get-tuple-element.105), channel_id=1, source_target_pairs={{0,4},{4,8},{8,12},{12,16},{16,20},{20,24},{24,28},{1,5},{5,9},{9,... | collective-permute-start | bytes 36872 | tf_op jit(solution)/shard_map/ppermute | solution.py:18
  96.8 5.6 %collective-permute-start.9 = (f32[3,8,1,128]{3,2,1,0:T(1,128)S(1)}, f32[3,8,1,128]{3,2,1,0:T(1,128)S(1)}, u32[]{:S(2)}, u32[]{:S(2)}) collective-permute-start(f32[3,8,1,128]{3,2,1,0:T(1,128)S(1)} %get-tuple-element.106), channel_id=1, source_target_pairs={{4,0},{8,4},{12,8},{16,12},{20,16},{24,20},{28,24},{5,1},{9,5},{13... | collective-permute-start | bytes 36872 | tf_op jit(solution)/shard_map/ppermute | solution.py:20
  102.6 8.4 %collective-permute-start.10 = (f32[3,8,18,1]{3,2,1,0:T(8,128)S(1)}, f32[3,8,18,1]{3,2,1,0:T(8,128)S(1)}, u32[]{:S(2)}, u32[]{:S(2)}) collective-permute-start(f32[3,8,18,1]{3,2,1,0:T(8,128)S(1)} %get-tuple-element.81), channel_id=1, source_target_pairs={{0,1},{1,2},{2,3},{4,5},{5,6},{6,7},{8,9},{9,10},{10,11},{12,13},{... | collective-permute-start | bytes 5192 | tf_op jit(solution)/shard_map/ppermute | solution.py:18
  107.3 8.0 %collective-permute-start.11 = (f32[3,8,18,1]{3,2,1,0:T(8,128)S(1)}, f32[3,8,18,1]{3,2,1,0:T(8,128)S(1)}, u32[]{:S(2)}, u32[]{:S(2)}) collective-permute-start(f32[3,8,18,1]{3,2,1,0:T(8,128)S(1)} %get-tuple-element.82), channel_id=1, source_target_pairs={{1,0},{2,1},{3,2},{5,4},{6,5},{7,6},{9,8},{10,9},{11,10},{13,12},{... | collective-permute-start | bytes 5192 | tf_op jit(solution)/shard_map/ppermute | solution.py:20
  115.9 0.9 copy-start.13
  117.0 0.9 copy-start.1
  (4 other events, 2.6 us)
where the time goes:
time: 121 us; the launch traced here: 120 us
  starting transfers between devices  42 us (35%)
  waiting for transfers between devices  27.7 us (23%)
  local copies, waits for them, and re-layouts  24.9 us (21%)
  other arithmetic  21.3 us (18%)
  matrix products  2.33 us (2%)
  between operations  1.77 us (1%)
    ppermute x6, starting transfers between devices, padded_2(): lax.ppermute(tail, axis, [(i, (i + 1) % count) for i in range(ends)])  23.5 us
    ppermute x6, waiting for transfers between devices, padded_2(): lax.ppermute(head, axis, [((i + 1) % count, i) for i in range(ends)])  18.5 us
    ppermute x6, starting transfers between devices, padded_2(): lax.ppermute(head, axis, [((i + 1) % count, i) for i in range(ends)])  12.1 us
    unnamed x113, local copies, waits for them, and re-layouts  10.6 us
    ppermute x6, waiting for transfers between devices, padded_2(): lax.ppermute(tail, axis, [(i, (i + 1) % count) for i in range(ends)])  9.19 us
    another operation x10, other arithmetic, operate(): return jnp.stack(components, axis=-4)  6.97 us
    all_to_all x1, starting transfers between devices, local(): lax.all_to_all(outgoing, ('gx', 'gy'), split_axis=0, concat_axis=0, tiled...  6.38 us
    slice x36, local copies, waits for them, and re-layouts, trimmed(): lax.slice_in_dim(values_in, head_cut, values_in.shape[axis_pos] - tail_cu...  4.89 us
  transfers between devices with their start and end apart: 13, of which 7 were waited for; matrix products, arithmetic and copies ran while one was open for 15% of the time, Pallas kernels for 0%

commit v1 on v0

v1 whole, which is shorter than its diff:
```python
import functools

import jax
import jax.numpy as jnp
from jax import lax
from jax.experimental import pallas as pl
from jax.experimental.pallas import tpu as pltpu
from jax.sharding import PartitionSpec as P

step_square = 0.05
time_weights = ((-0.0595, 0.7735, 0.3315, -0.0455), (-0.063756, 0.607068, 0.517132, -0.060444))

LANE = 128
WIDE = 256
VMEM = pltpu.VMEM
SMEM = pltpu.SMEM


def lane_ids(shape):
    return lax.broadcasted_iota(jnp.int32, shape, len(shape) - 1)


def sub_ids(shape):
    return lax.broadcasted_iota(jnp.int32, shape, len(shape) - 2)


def shift_up(u):
    count = u.shape[0]
    return jnp.where(sub_ids(u.shape) == count - 1, 0.0, pltpu.roll(u, count - 1, 0))


def shift_down(u):
    return jnp.where(sub_ids(u.shape) == 0, 0.0, pltpu.roll(u, 1, 0))


def shift_next(u):
    return pltpu.roll(u, u.shape[1] - 1, 1)


def shift_prior(u):
    return pltpu.roll(u, 1, 1)


def level_row(ref, plane, levels, rows, r):
    return ref[pl.ds(plane * levels * rows + r, levels, stride=rows), :]


def meta_vector(off_ref, rng_ref, groups):
    shape = (8, LANE)
    lane = lane_ids(shape)
    out = jnp.zeros(shape, jnp.float32)
    for g in range(groups):
        for q in range(3):
            out = jnp.where(lane == 3 * g + q, off_ref[0, 0, g, q].astype(jnp.float32), out)
    for q in range(2):
        out = jnp.where(lane == 3 * groups + q, rng_ref[0, 0, q].astype(jnp.float32), out)
    return out


def pre_kernel(
    lev, rows, groups, samples, coarse_ref, now_ref, prev_ref, dens_ref, mod_ref, off_ref, rng_ref,
    pay_ref, first_ref, last_ref, scr
):
    for k in range(coarse_ref.shape[0]):
        mixed = []
        for n in range(2):
            total = None
            for t in range(samples):
                term = time_weights[n][t] * coarse_ref[k, 6 * t : 6 * t + 6, :]
                total = term if total is None else total + term
            mixed.append(total)
        scr[8 * k : 8 * k + 6, :] = mixed[0]
        scr[8 * k + 6 : 8 * k + 8, :] = mixed[1][0:2]
        scr[16 + 4 * k : 20 + 4 * k, :] = mixed[1][2:6]
    head = [scr[8 * i : 8 * i + 8, :LANE] for i in range(3)]
    tail = [scr[8 * i : 8 * i + 8, LANE:] for i in range(3)]
    lane = lane_ids((8, LANE))
    tiles = head + [
        jnp.where(lane < 80, tail[0], pltpu.roll(tail[2], 80, 1)),
        jnp.where(lane < 80, tail[1], pltpu.roll(tail[2], 40, 1)),
    ]

    def send(d, carry):
        for i, tile in enumerate(tiles):
            pay_ref[d, 8 * i : 8 * i + 8, :] = tile
        return carry

    lax.fori_loop(0, pay_ref.shape[0], send, 0)
    meta = meta_vector(off_ref, rng_ref, groups)
    for ref, start, edge in ((first_ref, 0, 0), (last_ref, rows - 2, rows - 1)):
        for c in range(3):
            for r in range(2):
                ref[2 * c + r] = level_row(now_ref, c, lev, rows, start + r)
            ref[10 + c] = level_row(prev_ref, c, lev, rows, edge)
        for k in range(2):
            for r in range(2):
                ref[6 + 2 * k + r] = level_row(mod_ref, k, lev, rows, start + r)
        ref[13] = level_row(dens_ref, 0, lev, rows, edge)
        ref[14] = meta


def plane_row(refs, lev, rows, plane, x):
    now_ref, prev_ref, dens_ref, mod_ref, before_ref, after_ref = refs
    if plane < 3:
        source, own, strip, both = now_ref, plane, 2 * plane, True
    elif plane < 5:
        source, own, strip, both = mod_ref, plane - 3, 6 + 2 * (plane - 3), True
    elif plane < 8:
        source, own, strip, both = prev_ref, plane - 5, 10 + plane - 5, False
    else:
        source, own, strip, both = dens_ref, 0, 13, False
    if 2 <= x < rows + 2:
        return level_row(source, own, lev, rows, x - 2)
    ref, r = (before_ref, x) if x < 2 else (after_ref, x - rows - 2)
    if both:
        return ref[strip + r]
    return ref[strip] if x in (1, rows + 2) else None


def pack_kernel(
    lev, rows, groups, now_ref, prev_ref, dens_ref, mod_ref, before_ref, after_ref, off_ref, rng_ref,
    west_ref, east_ref, meta_ref
):
    refs = (now_ref, prev_ref, dens_ref, mod_ref, before_ref, after_ref)
    lane = lane_ids((lev, LANE))
    span = 2 * (rows + 4)
    for block in range(3):
        west = jnp.zeros((lev, LANE), jnp.float32)
        east = jnp.zeros((lev, LANE), jnp.float32)
        for p in range(3):
            for x in range(rows + 4):
                v = plane_row(refs, lev, rows, 3 * block + p, x)
                if v is None:
                    continue
                at = span * p + 2 * x
                here = (lane == at) | (lane == at + 1)
                west = jnp.where(here, pltpu.roll(v, at, 1), west)
                east = jnp.where(here, pltpu.roll(v, (at + 2) % LANE, 1), east)
        west_ref[block] = west
        east_ref[block] = east
    sub = sub_ids((lev, LANE))
    meta = meta_vector(off_ref, rng_ref, groups)
    both = jnp.where(sub == 0, before_ref[14], jnp.where(sub == 1, meta, after_ref[14]))
    west_ref[3] = both
    east_ref[3] = both
    meta_ref[...] = both


MU = {"l+": 0, "l-": 1, "e+": 2, "e-": 3, "n+": 4, "n-": 5}
STIFF = {"l+": 6, "l-": 7, "e+": 8, "e-": 9, "n+": 10, "n-": 11}
CENTER = 12
MU_QUARTER = 15
LAME_QUARTER = 16
COEFS = 17


def quarter_row(mod_ref, coef_ref, x):
    coef_ref[MU_QUARTER, x] = 0.25 * mod_ref[0, x]
    coef_ref[LAME_QUARTER, x] = 0.25 * mod_ref[1, x]


def coef_row(mod_ref, coef_ref, x):
    sums = []
    for stiff, table in ((False, MU), (True, STIFF)):

        def half(r):
            mu = mod_ref[0, r]
            return 0.5 * mod_ref[1, r] + mu if stiff else 0.5 * mu

        k = half(x)
        values = {
            "l+": k + shift_up(k),
            "l-": k + shift_down(k),
            "e+": k + half(x + 1),
            "e-": k + half(x - 1),
            "n+": k + shift_next(k),
            "n-": k + shift_prior(k),
        }
        for name, value in values.items():
            coef_ref[table[name], x] = value
        sums.append({d: values[d + "+"] + values[d + "-"] for d in "len"})
    soft, hard = sums
    coef_ref[CENTER + 0, x] = hard["l"] + soft["e"] + soft["n"]
    coef_ref[CENTER + 1, x] = soft["l"] + hard["e"] + soft["n"]
    coef_ref[CENTER + 2, x] = soft["l"] + soft["e"] + hard["n"]


def east_flow(u, coef_ref, x):
    mu = coef_ref[MU_QUARTER, x]
    lame = coef_ref[LAME_QUARTER, x]
    rise = [shift_up(u[c]) - shift_down(u[c]) for c in range(2)]
    run = [shift_next(u[c]) - shift_prior(u[c]) for c in (1, 2)]
    return mu * rise[1], lame * (rise[0] + run[1]), mu * run[0]


def apply_row(field, flow, coef_ref, x, width):
    def cut(v):
        return v[:, :width]

    u = [field(c, x) for c in range(3)]
    after = [field(c, x + 1) for c in range(3)]
    before = [field(c, x - 1) for c in range(3)]
    up = [shift_up(v) for v in u]
    down = [shift_down(v) for v in u]
    nxt = [shift_next(v) for v in u]
    prior = [shift_prior(v) for v in u]
    d_l = [up[c] - down[c] for c in range(3)]
    d_n = [nxt[c] - prior[c] for c in range(3)]
    d_e = [after[c] - before[c] for c in range(3)]
    mu = coef_ref[MU_QUARTER, x]
    lame = coef_ref[LAME_QUARTER, x]
    level_flow = (cut(lame * (d_e[1] + d_n[2])), cut(mu * d_e[0]), cut(mu * d_n[0]))
    north_flow = (mu * d_l[2], mu * d_e[2], lame * (d_l[0] + d_e[1]))
    out = []
    for i in range(3):

        def coef(name):
            table = STIFF if "len".index(name[0]) == i else MU
            return cut(coef_ref[table[name], x])

        total = cut(flow(i, x + 1)) - cut(flow(i, x - 1))
        total += shift_up(level_flow[i]) - shift_down(level_flow[i])
        total += cut(shift_next(north_flow[i]) - shift_prior(north_flow[i]))
        total += coef("l+") * cut(up[i]) + coef("l-") * cut(down[i])
        total += coef("e+") * cut(after[i]) + coef("e-") * cut(before[i])
        total += coef("n+") * cut(nxt[i]) + coef("n-") * cut(prior[i])
        total -= cut(coef_ref[CENTER + i, x]) * cut(u[i])
        out.append(total)
    return out


def prep_kernel(
    lev, rows, groups, c_north, now_ref, prev_ref, dens_ref, mod_ref, before_ref, after_ref, west_ref, east_ref, meta_ref,
    route_ref, place_ref, mods_ref, base_ref, scale_ref, mask_ref, level_ref, shift_ref, own_hat_ref, side_hat_ref,
    index_ref, now_x, flow, coef
):
    refs = (now_ref, prev_ref, dens_ref, mod_ref, before_ref, after_ref)
    lane = lane_ids((lev, LANE))
    sub = sub_ids((lev, LANE))
    span = 2 * (rows + 4)
    metas = (meta_ref[...], east_ref[3], west_ref[3])

    for i in range(9 * groups):
        index_ref[i] = 0
    my_x, my_y = place_ref[0], place_ref[1]
    n_y = place_ref[2]

    def find(b, carry):
        slot = route_ref[b]
        tile = lax.div(slot, groups)
        g = slot - tile * groups
        tile_x = lax.div(tile, n_y)
        d_x = tile_x - my_x + 1
        d_y = tile - tile_x * n_y - my_y
        column = jnp.where(d_y < 0, 2, d_y)

        @pl.when((d_x >= 0) & (d_x < 3) & (d_y >= -1) & (d_y < 2))
        def _():
            index_ref[(d_x * 3 + column) * groups + g] = b

        return carry

    lax.fori_loop(0, route_ref.shape[0], find, 0)

    def sides(plane, x):
        block, p = divmod(plane, 3)
        at = span * p + 2 * x
        return jnp.where(
            lane < 2,
            pltpu.roll(east_ref[block], (-at) % LANE, 1),
            jnp.where(lane >= LANE - 2, pltpu.roll(west_ref[block], (LANE - 2 - at) % LANE, 1), 0.0),
        )

    for x in range(rows + 4):
        for c in range(3):
            now_x[c, x, :, :LANE] = plane_row(refs, lev, rows, c, x)
            now_x[c, x, :, LANE:] = sides(c, x)
        for k in range(2):
            mods_ref[k, x, :, :LANE] = plane_row(refs, lev, rows, 3 + k, x)
            mods_ref[k, x, :, LANE:] = sides(3 + k, x)
        if 1 <= x < rows + 3:
            for c in range(3):
                base_ref[c, x, :, :LANE] = plane_row(refs, lev, rows, 5 + c, x)
                base_ref[c, x, :, LANE:] = sides(5 + c, x)
            for part, v in ((slice(0, LANE), plane_row(refs, lev, rows, 8, x)), (slice(LANE, WIDE), sides(8, x))):
                there = v > 0.0
                scale_ref[x, :, part] = jnp.where(there, step_square / jnp.where(there, v, 1.0), 0.0)

    def first(x, carry):
        quarter_row(mods_ref, coef, x)
        parts = east_flow([now_x[c, x] for c in range(3)], coef, x)
        for i in range(3):
            flow[i, x] = parts[i]
        return carry

    lax.fori_loop(0, rows + 4, first, 0)

    def second(x, carry):
        coef_row(mods_ref, coef, x)
        applied = apply_row(lambda c, r: now_x[c, r], lambda i, r: flow[i, r], coef, x, WIDE)
        for c in range(3):
            base_ref[c, x] = 2.0 * now_x[c, x] - base_ref[c, x] + scale_ref[x] * applied[c]
        return carry

    lax.fori_loop(1, rows + 3, second, 0)

    group_of_sub = sub // 2
    second_level = (sub - 2 * group_of_sub).astype(jnp.float32)
    k_row = sub_ids((LANE, LANE))
    k_lane = lane_ids((LANE, LANE))
    sub_f = sub.astype(jnp.float32)
    for t in range(3):
        def entry(column, i):
            return metas[column][t : t + 1, i : i + 1]

        for column in range(3):
            low = entry(column, 3 * groups)
            high = entry(column, 3 * groups + 1)
            outer = (sub_f < low).astype(jnp.float32)
            inner = ((sub_f >= low) & (sub_f < high)).astype(jnp.float32)
            if column == 0:
                mask_ref[0, t, :, :LANE] = outer
                mask_ref[1, t, :, :LANE] = inner
            elif column == 1:
                east_masks = (outer, inner)
            else:
                for q, own in enumerate((outer, inner)):
                    mask_ref[q, t, :, LANE:] = jnp.where(lane < LANE // 2, east_masks[q], own)
            depth = second_level
            east_at = jnp.zeros((lev, LANE), jnp.float32)
            hold = jnp.zeros((lev, LANE), jnp.float32)
            north_at = jnp.zeros((LANE, LANE), jnp.float32)
            point = jnp.zeros((LANE, LANE), jnp.float32)
            for g in range(groups):
                here = group_of_sub == g
                depth = jnp.where(here, second_level + entry(column, 3 * g), depth)
                east_at = jnp.where(here, 4.0 * entry(column, 3 * g + 1), east_at)
                mine = here & (lane >= g * c_north) & (lane < (g + 1) * c_north)
                hold = jnp.where(mine & (high > 2.0 * g + 1.0), 1.0 / 625.0, hold)
                there = (k_row >= g * c_north) & (k_row < (g + 1) * c_north)
                north_at = jnp.where(there, 4.0 * entry(column, 3 * g + 2), north_at)
                point = jnp.where(there, 25.0 * (k_row - g * c_north).astype(jnp.float32), point)
            depth = depth * (4.0 / 25.0)
            level_ref[t, column, 0] = hold * (1.0 - depth)
            level_ref[t, column, 1] = hold * depth
            hat = jnp.maximum(25.0 - jnp.abs(north_at + 4.0 * k_lane.astype(jnp.float32) - point), 0.0)
            hat = jnp.where(k_row < groups * c_north, hat, 0.0)
            if column == 0:
                shift_ref[t, :, :LANE] = east_at
                own_hat_ref[t] = hat.astype(jnp.bfloat16)
            elif column == 1:
                east_shift = east_at
                side_hat_ref[t, :LANE, :] = jnp.where(k_lane < LANE // 2, hat, 0.0).astype(jnp.bfloat16)
            else:
                shift_ref[t, :, LANE:] = jnp.where(lane < LANE // 2, east_shift, east_at)
                side_hat_ref[t, LANE:, :] = jnp.where(k_lane >= LANE // 2, hat, 0.0).astype(jnp.bfloat16)


def split_dot(ref, hat):
    v = ref[...]
    high = v.astype(jnp.bfloat16)
    low = (v - high.astype(jnp.float32)).astype(jnp.bfloat16)
    return jnp.dot(high, hat, preferred_element_type=jnp.float32) + jnp.dot(
        low, hat, preferred_element_type=jnp.float32
    )


def finish_kernel(
    lev, rows, groups, c_east, c_north, block_hold, got_ref, index_ref, mods_ref, base_ref, scale_ref, mask_ref,
    level_ref, shift_ref, own_hat_ref, side_hat_ref, now_ref, inc_out, mid_out, next_out,
    mixed, own_rows, side_rows, north, parts, flow, mid, coef
):
    lane = lane_ids((8, LANE))

    def quarter(x, carry):
        quarter_row(mods_ref, coef, x)
        return carry

    lax.fori_loop(0, rows + 4, quarter, 0)

    def coefs(x, carry):
        coef_row(mods_ref, coef, x)
        return carry

    lax.fori_loop(1, rows + 3, coefs, 0)

    def tile_row(t, carry):
        for column in range(3):
            pieces = []
            for g in range(groups):
                b = index_ref[(t * 3 + column) * groups + g]
                source = lax.div(b, block_hold)
                k = b - source * block_hold
                top = pl.multiple_of(8 * k, 8)
                third = got_ref[source, 24:32, :]
                fourth = got_ref[source, 32:40, :]
                tail = jnp.where(lane < 40, pltpu.roll(third, LANE - 80, 1), pltpu.roll(fourth, LANE - 40, 1))
                pieces.append(
                    (
                        (got_ref[source, pl.ds(top, 8), :], got_ref[source, pl.ds(24 + top, 8), :]),
                        (pltpu.roll(got_ref[source, 16:24, :], 4 * k, 0), pltpu.roll(tail, 4 * k, 0)),
                    )
                )
            for a in range(c_east):
                start = a * c_north
                for half in range(2):
                    total = jnp.zeros((8, LANE), jnp.float32)
                    for g in range(groups):
                        body, tail = pieces[g][half]
                        at = g * c_north
                        if start + c_north <= LANE:
                            moved = pltpu.roll(body, (at - start) % LANE, 1)
                        elif start >= LANE:
                            moved = pltpu.roll(tail, (at - start) % LANE, 1)
                        else:
                            moved = jnp.where(
                                lane < at + LANE - start,
                                pltpu.roll(body, (at - start) % LANE, 1),
                                pltpu.roll(tail, (at - start) % LANE, 1),
                            )
                        total = jnp.where((lane >= at) & (lane < at + c_north), moved, total)
                    mixed[a, 8 * half : 8 * half + 8, :] = total
            w0 = level_ref[t, column, 0]
            w1 = level_ref[t, column, 1]
            for nc in range(6):
                r = (nc // 3) * 6 + 2 * (nc % 3)
                for a in range(c_east):
                    value = w0 * jnp.broadcast_to(mixed[a, r : r + 1, :], (lev, LANE)) + w1 * jnp.broadcast_to(
                        mixed[a, r + 1 : r + 2, :], (lev, LANE)
                    )
                    at = (nc * c_east + a) * lev
                    if column == 0:
                        own_rows[at : at + lev, :] = value
                    elif column == 1:
                        side_rows[at : at + lev, :LANE] = value
                    else:
                        side_rows[at : at + lev, LANE:] = value
        own = split_dot(own_rows, own_hat_ref[t])
        north[t, :, :, :LANE] = own.reshape(6 * c_east, lev, LANE)
        side = split_dot(side_rows, side_hat_ref[t])
        north[t, :, :, LANE:] = side.reshape(6 * c_east, lev, LANE)
        return carry

    lax.fori_loop(0, 3, tile_row, 0)

    near = (4 * 24) // 25 + 3

    def east(x, carry):
        t = (x >= 2).astype(jnp.int32) + (x >= rows + 2).astype(jnp.int32)
        cell = x - 2 + rows - t * rows
        first = lax.div(4 * cell, 25)
        at = shift_ref[t] + (4 * cell - 25 * first).astype(jnp.float32)
        weights = [jnp.maximum(25.0 - jnp.abs(at - 25.0 * i), 0.0) for i in range(near)]
        outer = mask_ref[0, t]
        inner = mask_ref[1, t]
        values = []
        for nc in range(6):
            total = None
            for i in range(near):
                term = weights[i] * north[t, nc * c_east + first + i]
                total = term if total is None else total + term
            values.append(total)
            parts[nc, x] = outer * total
            parts[6 + nc, x] = inner * total

        @pl.when(t == 1)
        def _():
            for nc in range(6):
                inc_out[pl.ds(nc * lev * rows + cell, lev, stride=rows), :] = values[nc][:, :LANE]

        for q, mask in enumerate((outer, inner)):
            moved = east_flow([mask * values[c] for c in range(3)], coef, x)
            for i in range(3):
                flow[3 * q + i, x] = moved[i]
        return carry

    lax.fori_loop(0, rows + 4, east, 0)

    def forcing(step, x, t, width):
        outside = apply_row(
            lambda c, r: parts[3 * step + c, r], lambda i, r: flow[i, r], coef, x, width
        )
        inside = apply_row(
            lambda c, r: parts[6 + 3 * step + c, r], lambda i, r: flow[3 + i, r], coef, x, width
        )
        outer = mask_ref[0, t][:, :width]
        inner = mask_ref[1, t][:, :width]
        return [inner * outside[c] - outer * inside[c] for c in range(3)]

    def middle(x, carry):
        t = (x >= 2).astype(jnp.int32) + (x >= rows + 2).astype(jnp.int32)
        force = forcing(0, x, t, WIDE)
        for c in range(3):
            mid[c, x] = base_ref[c, x] + scale_ref[x] * force[c]
        return carry

    lax.fori_loop(1, rows + 3, middle, 0)

    def flows(x, carry):
        for q, load in enumerate(
            (lambda c: parts[3 + c, x], lambda c: parts[9 + c, x], lambda c: mid[c, x])
        ):
            moved = east_flow([load(c) for c in range(3)], coef, x)
            for i in range(3):
                flow[3 * q + i, x] = moved[i]
        return carry

    lax.fori_loop(1, rows + 3, flows, 0)

    def last(x, carry):
        force = forcing(1, x, 1, LANE)
        applied = apply_row(lambda c, r: mid[c, r], lambda i, r: flow[6 + i, r], coef, x, LANE)
        scale = scale_ref[x, :, :LANE]
        for c in range(3):
            now = now_ref[pl.ds(c * lev * rows + x - 2, lev, stride=rows), :]
            current = mid[c, x, :, :LANE]
            mid_out[pl.ds(c * lev * rows + x - 2, lev, stride=rows), :] = current
            next_out[pl.ds(c * lev * rows + x - 2, lev, stride=rows), :] = (
                2.0 * current - now + scale * (applied[c] + force[c])
            )
        return carry

    lax.fori_loop(2, rows + 2, last, 0)


def specs(text):
    space = {"v": VMEM, "s": SMEM}
    return [pl.BlockSpec(memory_space=space[kind]) for kind in text]


def f32(*shape):
    return jax.ShapeDtypeStruct(shape, jnp.float32)


def neighbours(axis, step):
    count = lax.axis_size(axis)
    return [(i, i + step) for i in range(count) if 0 <= i + step < count]


def local(disp_now, disp_prev, density, moduli, coarse, block_route, ranges, offsets):
    _, lev, rows, north_cells = disp_now.shape
    groups = lev // 2
    c_east = (rows + 23) * 4 // 25 + 2
    c_north = (north_cells + 23) * 4 // 25 + 2
    block_hold = coarse.shape[0]
    samples = coarse.shape[1] // 6
    n_x = lax.axis_size("gx")
    n_y = lax.axis_size("gy")
    assert lev == 8 and north_cells == LANE and block_hold == 2
    assert (c_east, c_north) == (8, 26) and 6 * (rows + 4) <= LANE
    now, prev, dens, mods = (a.reshape(-1, north_cells) for a in (disp_now, disp_prev, density, moduli))
    wide = rows + 4

    payload, first, last = pl.pallas_call(
        functools.partial(pre_kernel, lev, rows, groups, samples),
        out_shape=(f32(n_x * n_y, 40, LANE), f32(15, lev, LANE), f32(15, lev, LANE)),
        in_specs=specs("vvvvvss"),
        out_specs=specs("vvv"),
        scratch_shapes=[VMEM((24, WIDE), jnp.float32)],
        name="pre",
    )(coarse, now, prev, dens, mods, offsets, ranges)
    got = lax.all_to_all(payload, ("gx", "gy"), split_axis=0, concat_axis=0, tiled=True)
    before = lax.ppermute(last, "gx", neighbours("gx", 1))
    after = lax.ppermute(first, "gx", neighbours("gx", -1))
    to_west, to_east, meta = pl.pallas_call(
        functools.partial(pack_kernel, lev, rows, groups),
        out_shape=(f32(4, lev, LANE), f32(4, lev, LANE), f32(lev, LANE)),
        in_specs=specs("vvvvvvss"),
        out_specs=specs("vvv"),
        cost_estimate=pl.CostEstimate(flops=2000000, bytes_accessed=1000000, transcendentals=0),
        name="pack",
    )(now, prev, dens, mods, before, after, offsets, ranges)
    west = lax.ppermute(to_east, "gy", neighbours("gy", 1))
    east = lax.ppermute(to_west, "gy", neighbours("gy", -1))
    place = jnp.stack([lax.axis_index("gx"), lax.axis_index("gy"), jnp.int32(n_y)]).astype(jnp.int32)
    prepared = pl.pallas_call(
        functools.partial(prep_kernel, lev, rows, groups, c_north),
        out_shape=(
            f32(2, wide, lev, WIDE),
            f32(3, wide, lev, WIDE),
            f32(wide, lev, WIDE),
            f32(2, 3, lev, WIDE),
            f32(3, 3, 2, lev, LANE),
            f32(3, lev, WIDE),
            jax.ShapeDtypeStruct((3, LANE, LANE), jnp.bfloat16),
            jax.ShapeDtypeStruct((3, WIDE, LANE), jnp.bfloat16),
            jax.ShapeDtypeStruct((9 * groups,), jnp.int32),
        ),
        in_specs=specs("vvvvvvvvvss"),
        out_specs=specs("vvvvvvvvs"),
        scratch_shapes=[
            VMEM((3, wide, lev, WIDE), jnp.float32),
            VMEM((3, wide, lev, WIDE), jnp.float32),
            VMEM((COEFS, wide, lev, WIDE), jnp.float32),
        ],
        cost_estimate=pl.CostEstimate(flops=10000000, bytes_accessed=3000000, transcendentals=0),
        name="prep",
    )(now, prev, dens, mods, before, after, west, east, meta, block_route, place)
    mods_x, base, scale, mask, level_w, shift, own_hat, side_hat, index = prepared
    incident, mid, nxt = pl.pallas_call(
        functools.partial(finish_kernel, lev, rows, groups, c_east, c_north, block_hold),
        out_shape=(
            f32(6 * lev * rows, LANE),
            f32(3 * lev * rows, LANE),
            f32(3 * lev * rows, LANE),
        ),
        in_specs=specs("vsvvvvvvvvv"),
        out_specs=specs("vvv"),
        scratch_shapes=[
            VMEM((c_east, 16, LANE), jnp.float32),
            VMEM((6 * c_east * lev, LANE), jnp.float32),
            VMEM((6 * c_east * lev, WIDE), jnp.float32),
            VMEM((3, 6 * c_east, lev, WIDE), jnp.float32),
            VMEM((12, wide, lev, WIDE), jnp.float32),
            VMEM((9, wide, lev, WIDE), jnp.float32),
            VMEM((3, wide, lev, WIDE), jnp.float32),
            VMEM((COEFS, wide, lev, WIDE), jnp.float32),
        ],
        cost_estimate=pl.CostEstimate(flops=20000000, bytes_accessed=6000000, transcendentals=0),
        name="finish",
    )(got, index, mods_x, base, scale, mask, level_w, shift, own_hat, side_hat, now)
    return (
        incident.reshape(2, 3, lev, rows, north_cells),
        mid.reshape(disp_now.shape),
        nxt.reshape(disp_now.shape),
    )


def solution(mesh):
    return jax.shard_map(
        local,
        mesh=mesh,
        in_specs=(
            P(None, None, "gx", "gy"),
            P(None, None, "gx", "gy"),
            P(None, "gx", "gy"),
            P(None, None, "gx", "gy"),
            P(("gx", "gy"), None, None),
            P(),
            P("gx", "gy", None),
            P("gx", "gy", None, None),
        ),
        out_specs=(
            P(None, None, None, "gx", "gy"),
            P(None, None, "gx", "gy"),
            P(None, None, "gx", "gy"),
        ),
        check_vma=False,
    )
```

time: 121 us -> 65.4 us (0.54)
  the two profiles are of different devices: /device:TPU:5 before, /device:TPU:17 now
where the time goes in v1:
time: 65.4 us; the launch traced here: 65 us
  Pallas kernels  27.6 us (42%)
  starting transfers between devices  17.8 us (27%)
  waiting for transfers between devices  14.3 us (22%)
  local copies, waits for them, and re-layouts  4.03 us (6%)
  between operations  0.72 us (1%)
    pallas_call x1, Pallas kernels, local(): pl.pallas_call(functools.partial(finish_kernel, lev, rows, groups, c_east...  14.7 us
    ppermute x1, waiting for transfers between devices, local(): before = lax.ppermute(last, 'gx', neighbours('gx', 1))  11.5 us
    pallas_call x1, Pallas kernels, local(): pl.pallas_call(functools.partial(prep_kernel, lev, rows, groups, c_north)...  8.41 us
    all_to_all x1, starting transfers between devices, local(): lax.all_to_all(payload, ('gx', 'gy'), split_axis=0, concat_axis=0, tiled=...  6.22 us
    unnamed x15, local copies, waits for them, and re-layouts  4.03 us
    ppermute x1, starting transfers between devices, local(): west = lax.ppermute(to_east, 'gy', neighbours('gy', 1))  3.5 us
    ppermute x1, starting transfers between devices, local(): before = lax.ppermute(last, 'gx', neighbours('gx', 1))  3.11 us
    ppermute x1, starting transfers between devices, local(): after = lax.ppermute(first, 'gx', neighbours('gx', -1))  3.07 us
  transfers between devices with their start and end apart: 5, of which 2 were waited for; matrix products, arithmetic and copies ran while one was open for 1% of the time, Pallas kernels for 16%

profile of v1, /device:TPU:17, one launch (start us, length us, event | category | flops | bytes accessed | tf_op | source)
XLA Modules:
  0.0 65.0 jit_solution(9057081135685097046)
XLA Ops:
  0.6 1.3 %copy.11.off_ref = s32[1,1,4,3]{3,2,1,0:T(4,128)} copy(s32[1,1,4,3]{2,1,3,0:T(1,128)} %param.15) | data formatting | bytes 96 | tf_op args[7]
  2.0 2.3 %pre.1 = (f32[32,40,128]{2,1,0:T(8,128)}, f32[15,8,128]{2,1,0:T(8,128)}, f32[15,8,128]{2,1,0:T(8,128)}) custom-call(f32[2,24,256]{2,1,0:T(8,128)} %coarse_ref.1, f32[384,128]{1,0:T(8,128)} %bitcast.9, f32[384,128]{1,0:T(8,128)} %bitcast.13, f32[128,128]{1,0:T(8,128)} %bitcast.19, f32[256,128]{1,0:T(8,128)} %bitcast.16, s32[1,1,4,3]{3,2,1,0:T(4,128)} %copy.11.off_ref, ...), custom_call_target="tpu_custom_call" | custom-call | tf_op jit(solution)/shard_map/pre/pallas_call | solution.py:554
  4.3 0.0 copy-start.6
  4.3 0.0 copy-start.5
  4.3 6.2 %all-to-all-start = ((f32[32,40,128]{2,1,0:T(8,128)}), f32[32,40,128]{2,1,0:T(8,128)S(1)}, u32[]{:S(2)}, u32[]{:S(2)}) async-start(f32[32,40,128]{2,1,0:T(8,128)} %get-tuple-element.21), calls=%async_computation | async-start | bytes 1310720 | tf_op jit(solution)/shard_map/all_to_all | solution.py:562
  10.5 0.0 copy-done.6
  10.5 3.1 %collective-permute-start = (f32[15,8,128]{2,1,0:T(8,128)S(1)}, f32[15,8,128]{2,1,0:T(8,128)S(1)}, u32[]{:S(2)}, u32[]{:S(2)}) collective-permute-start(f32[15,8,128]{2,1,0:T(8,128)S(1)} %copy-done.6), channel_id=1, source_target_pairs={{0,4},{4,8},{8,12},{12,16},{16,20},{20,24},{24,28},{1,5},{5,9},{9,... | collective-permute-start | bytes 184328 | tf_op jit(solution)/shard_map/ppermute | solution.py:563
  13.6 0.0 copy-done.5
  13.6 3.1 %collective-permute-start.1 = (f32[15,8,128]{2,1,0:T(8,128)S(1)}, f32[15,8,128]{2,1,0:T(8,128)S(1)}, u32[]{:S(2)}, u32[]{:S(2)}) collective-permute-start(f32[15,8,128]{2,1,0:T(8,128)S(1)} %copy-done.5), channel_id=1, source_target_pairs={{4,0},{8,4},{12,8},{16,12},{20,16},{24,20},{28,24},{5,1},{9,5},{13... | collective-permute-start | bytes 184328 | tf_op jit(solution)/shard_map/ppermute | solution.py:564
  16.7 11.5 %collective-permute-done.before_ref = f32[15,8,128]{2,1,0:T(8,128)S(1)} collective-permute-done((f32[15,8,128]{2,1,0:T(8,128)S(1)}, f32[15,8,128]{2,1,0:T(8,128)S(1)}, u32[]{:S(2)}, u32[]{:S(2)}) %collective-permute-start) | collective-permute-done | bytes 61472 | tf_op jit(solution)/shard_map/ppermute | solution.py:563
  28.2 0.0 copy-start.1
  28.2 0.0 collective-permute-done.1.after_ref
  28.2 0.6 copy-done.1
  28.8 0.0 copy-start.2
  28.8 0.6 copy-done.2
  29.5 2.2 %pack.1 = (f32[4,8,128]{2,1,0:T(8,128)}, f32[4,8,128]{2,1,0:T(8,128)}, f32[8,128]{1,0:T(8,128)}) custom-call(f32[384,128]{1,0:T(8,128)} %bitcast.10, f32[384,128]{1,0:T(8,128)} %bitcast.14, f32[128,128]{1,0:T(8,128)} %bitcast.20, f32[256,128]{1,0:T(8,128)} %bitcast.17, f32[15,8,128]{2,1,0:T(8,128)} %copy-done.1, f32[15,8,128]{2,1,0:T(8,128)} %copy-done.2, ...), custom_call_target="tpu_custom_call" | custom-call | flops 2000000 | bytes 1000000 | tf_op jit(solution)/shard_map/pack/pallas_call | solution.py:565
  31.7 3.5 %collective-permute-start.2 = (f32[4,8,128]{2,1,0:T(8,128)}, f32[4,8,128]{2,1,0:T(8,128)S(1)}, u32[]{:S(2)}, u32[]{:S(2)}) collective-permute-start(f32[4,8,128]{2,1,0:T(8,128)} %get-tuple-element.24), channel_id=1, source_target_pairs={{0,1},{1,2},{2,3},{4,5},{5,6},{6,7},{8,9},{9,10},{10,11},{12,13},{... | collective-permute-start | bytes 49160 | tf_op jit(solution)/shard_map/ppermute | solution.py:573
  35.2 1.9 %collective-permute-start.3 = (f32[4,8,128]{2,1,0:T(8,128)}, f32[4,8,128]{2,1,0:T(8,128)S(1)}, u32[]{:S(2)}, u32[]{:S(2)}) collective-permute-start(f32[4,8,128]{2,1,0:T(8,128)} %get-tuple-element.25), channel_id=1, source_target_pairs={{1,0},{2,1},{3,2},{5,4},{6,5},{7,6},{9,8},{10,9},{11,10},{13,12},{... | collective-permute-start | bytes 49160 | tf_op jit(solution)/shard_map/ppermute | solution.py:574
  37.1 0.6 pad_add_fusion.place_ref
  37.7 0.0 collective-permute-done.2.west_ref
  37.7 0.0 copy-start.3
  37.7 2.7 %collective-permute-done.3.east_ref = f32[4,8,128]{2,1,0:T(8,128)S(1)} collective-permute-done((f32[4,8,128]{2,1,0:T(8,128)}, f32[4,8,128]{2,1,0:T(8,128)S(1)}, u32[]{:S(2)}, u32[]{:S(2)}) %collective-permute-start.3) | collective-permute-done | bytes 16416 | tf_op jit(solution)/shard_map/ppermute | solution.py:574
  40.4 0.0 copy-start.4
  40.4 0.0 copy-done.3
  40.4 0.6 copy-done.4
  41.0 8.4 %prep.1 = (f32[2,20,8,256]{3,2,1,0:T(8,128)}, f32[3,20,8,256]{3,2,1,0:T(8,128)}, f32[20,8,256]{2,1,0:T(8,128)}, f32[2,3,8,256]{3,2,1,0:T(8,128)}, f32[3,3,2,8,12...) custom-call(f32[384,128]{1,0:T(8,128)} %bitcast.11, ...), custom_call_target="tpu_custom_call" | custom-call | flops 10000000 | bytes 3000000 | tf_op jit(solution)/shard_map/prep/pallas_call | solution.py:576
  49.5 0.0 all-to-all-done.got_ref
  49.5 0.0 copy-start
  49.5 0.8 %copy-done = f32[32,40,128]{2,1,0:T(8,128)} copy-done((f32[32,40,128]{2,1,0:T(8,128)}, f32[32,40,128]{2,1,0:T(8,128)S(1)}, u32[]{:S(2)}) %copy-start) | copy-done | bytes 655384
  50.3 14.7 %finish.1 = (f32[768,128]{1,0:T(8,128)}, f32[384,128]{1,0:T(8,128)}, f32[384,128]{1,0:T(8,128)}) custom-call(f32[32,40,128]{2,1,0:T(8,128)} %copy-done, s32[36]{0:T(128)} %get-tuple-element.27.index_ref, f32[2,20,8,256]{3,2,1,0:T(8,128)} %get-tuple-element.28.mods_ref, f32[3,20,8,256]{3,2,1,0:T(8,128)} %get-tuple-element.29.base_ref, ...), custom_call_target="tpu_custom_call" | custom-call | flops 20000000 | bytes 6000000 | tf_op jit(solution)/shard_map/finish/pallas_call | solution.py:600
Async XLA Ops:
  4.3 6.2 %copy-start.6 = (f32[15,8,128]{2,1,0:T(8,128)S(1)}, f32[15,8,128]{2,1,0:T(8,128)}, u32[]{:S(2)}) copy-start(f32[15,8,128]{2,1,0:T(8,128)} %get-tuple-element.22) | copy-start | bytes 184324
  4.3 9.4 %copy-start.5 = (f32[15,8,128]{2,1,0:T(8,128)S(1)}, f32[15,8,128]{2,1,0:T(8,128)}, u32[]{:S(2)}) copy-start(f32[15,8,128]{2,1,0:T(8,128)} %get-tuple-element.23) | copy-start | bytes 184324
  4.3 45.2 %all-to-all-start = ((f32[32,40,128]{2,1,0:T(8,128)}), f32[32,40,128]{2,1,0:T(8,128)S(1)}, u32[]{:S(2)}, u32[]{:S(2)}) async-start(f32[32,40,128]{2,1,0:T(8,128)} %get-tuple-element.21), calls=%async_computation | async-start | bytes 1310720 | tf_op jit(solution)/shard_map/all_to_all | solution.py:562
  10.5 17.7 %collective-permute-start = (f32[15,8,128]{2,1,0:T(8,128)S(1)}, f32[15,8,128]{2,1,0:T(8,128)S(1)}, u32[]{:S(2)}, u32[]{:S(2)}) collective-permute-start(f32[15,8,128]{2,1,0:T(8,128)S(1)} %copy-done.6), channel_id=1, source_target_pairs={{0,4},{4,8},{8,12},{12,16},{16,20},{20,24},{24,28},{1,5},{5,9},{9,... | collective-permute-start | bytes 184328 | tf_op jit(solution)/shard_map/ppermute | solution.py:563
  13.6 14.6 %collective-permute-start.1 = (f32[15,8,128]{2,1,0:T(8,128)S(1)}, f32[15,8,128]{2,1,0:T(8,128)S(1)}, u32[]{:S(2)}, u32[]{:S(2)}) collective-permute-start(f32[15,8,128]{2,1,0:T(8,128)S(1)} %copy-done.5), channel_id=1, source_target_pairs={{4,0},{8,4},{12,8},{16,12},{20,16},{24,20},{28,24},{5,1},{9,5},{13... | collective-permute-start | bytes 184328 | tf_op jit(solution)/shard_map/ppermute | solution.py:564
  28.2 0.6 copy-start.1
  28.8 0.6 copy-start.2
  31.7 6.0 %collective-permute-start.2 = (f32[4,8,128]{2,1,0:T(8,128)}, f32[4,8,128]{2,1,0:T(8,128)S(1)}, u32[]{:S(2)}, u32[]{:S(2)}) collective-permute-start(f32[4,8,128]{2,1,0:T(8,128)} %get-tuple-element.24), channel_id=1, source_target_pairs={{0,1},{1,2},{2,3},{4,5},{5,6},{6,7},{8,9},{9,10},{10,11},{12,13},{... | collective-permute-start | bytes 49160 | tf_op jit(solution)/shard_map/ppermute | solution.py:573
  35.2 5.3 %collective-permute-start.3 = (f32[4,8,128]{2,1,0:T(8,128)}, f32[4,8,128]{2,1,0:T(8,128)S(1)}, u32[]{:S(2)}, u32[]{:S(2)}) collective-permute-start(f32[4,8,128]{2,1,0:T(8,128)} %get-tuple-element.25), channel_id=1, source_target_pairs={{1,0},{2,1},{3,2},{5,4},{6,5},{7,6},{9,8},{10,9},{11,10},{13,12},{... | collective-permute-start | bytes 49160 | tf_op jit(solution)/shard_map/ppermute | solution.py:574
  37.7 2.8 %copy-start.3 = (f32[4,8,128]{2,1,0:T(8,128)}, f32[4,8,128]{2,1,0:T(8,128)S(1)}, u32[]{:S(2)}) copy-start(f32[4,8,128]{2,1,0:T(8,128)S(1)} %collective-permute-done.2.west_ref) | copy-start | bytes 49156
  40.4 0.6 copy-start.4
  49.5 0.8 %copy-start = (f32[32,40,128]{2,1,0:T(8,128)}, f32[32,40,128]{2,1,0:T(8,128)S(1)}, u32[]{:S(2)}) copy-start(f32[32,40,128]{2,1,0:T(8,128)S(1)} %all-to-all-done.got_ref) | copy-start | bytes 1966084

commit v2 on v1

--- a/solution.py
+++ b/solution.py
@@ -7,6 +7,7 @@
 from jax.experimental.pallas import tpu as pltpu
 from jax.sharding import PartitionSpec as P
 
+
 step_square = 0.05
 time_weights = ((-0.0595, 0.7735, 0.3315, -0.0455), (-0.063756, 0.607068, 0.517132, -0.060444))
 
@@ -43,6 +44,17 @@
 
 def level_row(ref, plane, levels, rows, r):
     return ref[pl.ds(plane * levels * rows + r, levels, stride=rows), :]
+
+
+def rows_loop(start, stop, most, body):
+    step = max(d for d in range(1, most + 1) if (stop - start) % d == 0)
+
+    def chunk(i, carry):
+        for r in range(step):
+            body(start + i * step + r)
+        return carry
+
+    lax.fori_loop(0, (stop - start) // step, chunk, 0)
 
 
 def meta_vector(off_ref, rng_ref, groups):
@@ -51,16 +63,22 @@
     out = jnp.zeros(shape, jnp.float32)
     for g in range(groups):
         for q in range(3):
-            out = jnp.where(lane == 3 * g + q, off_ref[0, 0, g, q].astype(jnp.float32), out)
+            out = jnp.where(lane == 3 * g + q, off_ref[0, q, 0, g].astype(jnp.float32), out)
     for q in range(2):
         out = jnp.where(lane == 3 * groups + q, rng_ref[0, 0, q].astype(jnp.float32), out)
     return out
 
 
 def pre_kernel(
-    lev, rows, groups, samples, coarse_ref, now_ref, prev_ref, dens_ref, mod_ref, off_ref, rng_ref,
-    pay_ref, first_ref, last_ref, scr
+    lev, rows, groups, samples, *refs
 ):
+    sources, (off_ref, rng_ref, pay_ref, first_ref, last_ref, scr) = refs[:5], refs[5:11]
+    held, sems = refs[11:16], refs[16]
+    copies = [pltpu.make_async_copy(sources[i], held[i], sems.at[i]) for i in range(5)]
+    for copy in copies:
+        copy.start()
+    coarse_ref, now_ref, prev_ref, dens_ref, mod_ref = held
+    copies[0].wait()
     for k in range(coarse_ref.shape[0]):
         mixed = []
         for n in range(2):
@@ -80,13 +98,11 @@
         jnp.where(lane < 80, tail[1], pltpu.roll(tail[2], 40, 1)),
     ]
 
-    def send(d, carry):
-        for i, tile in enumerate(tiles):
-            pay_ref[d, 8 * i : 8 * i + 8, :] = tile
-        return carry
-
-    lax.fori_loop(0, pay_ref.shape[0], send, 0)
+    for i, tile in enumerate(tiles):
+        pay_ref[8 * i : 8 * i + 8, :] = tile
     meta = meta_vector(off_ref, rng_ref, groups)
+    for copy in copies[1:]:
+        copy.wait()
     for ref, start, edge in ((first_ref, 0, 0), (last_ref, rows - 2, rows - 1)):
         for c in range(3):
             for r in range(2):
@@ -230,7 +246,7 @@
 
 
 def prep_kernel(
-    lev, rows, groups, c_north, now_ref, prev_ref, dens_ref, mod_ref, before_ref, after_ref, west_ref, east_ref, meta_ref,
+    lev, rows, groups, c_north, n_x, n_y, now_ref, prev_ref, dens_ref, mod_ref, before_ref, after_ref, west_ref, east_ref, meta_ref,
     route_ref, place_ref, mods_ref, base_ref, scale_ref, mask_ref, level_ref, shift_ref, own_hat_ref, side_hat_ref,
     index_ref, now_x, flow, coef
 ):
@@ -243,7 +259,8 @@
     for i in range(9 * groups):
         index_ref[i] = 0
     my_x, my_y = place_ref[0], place_ref[1]
-    n_y = place_ref[2]
+    half = n_x * n_y // 2
+    upper = (2 * my_x >= n_x).astype(jnp.int32)
 
     def find(b, carry):
         slot = route_ref[b]
@@ -256,7 +273,10 @@
 
         @pl.when((d_x >= 0) & (d_x < 3) & (d_y >= -1) & (d_y < 2))
         def _():
-            index_ref[(d_x * 3 + column) * groups + g] = b
+            source = lax.div(b, 2)
+            far = (source >= half).astype(jnp.int32)
+            seat = 2 * (source - far * half) + (far ^ upper)
+            index_ref[(d_x * 3 + column) * groups + g] = 2 * seat + b - 2 * source
 
         return carry
 
@@ -286,23 +306,21 @@
                 there = v > 0.0
                 scale_ref[x, :, part] = jnp.where(there, step_square / jnp.where(there, v, 1.0), 0.0)
 
-    def first(x, carry):
+    def first(x):
         quarter_row(mods_ref, coef, x)
         parts = east_flow([now_x[c, x] for c in range(3)], coef, x)
         for i in range(3):
             flow[i, x] = parts[i]
-        return carry
-
-    lax.fori_loop(0, rows + 4, first, 0)
-
-    def second(x, carry):
-        coef_row(mods_ref, coef, x)
+
+    rows_loop(0, rows + 4, 5, first)
+    rows_loop(1, rows + 3, 6, lambda x: coef_row(mods_ref, coef, x))
+
+    def second(x):
         applied = apply_row(lambda c, r: now_x[c, r], lambda i, r: flow[i, r], coef, x, WIDE)
         for c in range(3):
             base_ref[c, x] = 2.0 * now_x[c, x] - base_ref[c, x] + scale_ref[x] * applied[c]
-        return carry
-
-    lax.fori_loop(1, rows + 3, second, 0)
+
+    rows_loop(1, rows + 3, 3, second)
 
     group_of_sub = sub // 2
     second_level = (sub - 2 * group_of_sub).astype(jnp.float32)
@@ -366,31 +384,21 @@
 
 
 def finish_kernel(
-    lev, rows, groups, c_east, c_north, block_hold, got_ref, index_ref, mods_ref, base_ref, scale_ref, mask_ref,
+    lev, rows, groups, c_east, c_north, got_ref, index_ref, mods_ref, base_ref, scale_ref, mask_ref,
     level_ref, shift_ref, own_hat_ref, side_hat_ref, now_ref, inc_out, mid_out, next_out,
     mixed, own_rows, side_rows, north, parts, flow, mid, coef
 ):
     lane = lane_ids((8, LANE))
-
-    def quarter(x, carry):
-        quarter_row(mods_ref, coef, x)
-        return carry
-
-    lax.fori_loop(0, rows + 4, quarter, 0)
-
-    def coefs(x, carry):
-        coef_row(mods_ref, coef, x)
-        return carry
-
-    lax.fori_loop(1, rows + 3, coefs, 0)
+    rows_loop(0, rows + 4, 5, lambda x: quarter_row(mods_ref, coef, x))
+    rows_loop(1, rows + 3, 6, lambda x: coef_row(mods_ref, coef, x))
 
     def tile_row(t, carry):
         for column in range(3):
             pieces = []
             for g in range(groups):
                 b = index_ref[(t * 3 + column) * groups + g]
-                source = lax.div(b, block_hold)
-                k = b - source * block_hold
+                source = b >> 1
+                k = b & 1
                 top = pl.multiple_of(8 * k, 8)
                 third = got_ref[source, 24:32, :]
                 fourth = got_ref[source, 32:40, :]
@@ -445,11 +453,10 @@
 
     near = (4 * 24) // 25 + 3
 
-    def east(x, carry):
-        t = (x >= 2).astype(jnp.int32) + (x >= rows + 2).astype(jnp.int32)
-        cell = x - 2 + rows - t * rows
-        first = lax.div(4 * cell, 25)
-        at = shift_ref[t] + (4 * cell - 25 * first).astype(jnp.float32)
+    def east(x, t, cell):
+        first = 4 * cell // 25 if isinstance(cell, int) else lax.div(4 * cell, 25)
+        ahead = 4 * cell - 25 * first
+        at = shift_ref[t] + (float(ahead) if isinstance(cell, int) else ahead.astype(jnp.float32))
         weights = [jnp.maximum(25.0 - jnp.abs(at - 25.0 * i), 0.0) for i in range(near)]
         outer = mask_ref[0, t]
         inner = mask_ref[1, t]
@@ -462,19 +469,17 @@
             values.append(total)
             parts[nc, x] = outer * total
             parts[6 + nc, x] = inner * total
-
-        @pl.when(t == 1)
-        def _():
-            for nc in range(6):
-                inc_out[pl.ds(nc * lev * rows + cell, lev, stride=rows), :] = values[nc][:, :LANE]
-
+            if not isinstance(cell, int):
+                inc_out[pl.ds(nc * lev * rows + cell, lev, stride=rows), :] = total[:, :LANE]
         for q, mask in enumerate((outer, inner)):
             moved = east_flow([mask * values[c] for c in range(3)], coef, x)
             for i in range(3):
                 flow[3 * q + i, x] = moved[i]
-        return carry
-
-    lax.fori_loop(0, rows + 4, east, 0)
+
+    rows_loop(0, rows, 4, lambda cell: east(cell + 2, 1, cell))
+    for r in range(2):
+        east(r, 0, rows - 2 + r)
+        east(rows + 2 + r, 2, r)
 
     def forcing(step, x, t, width):
         outside = apply_row(
@@ -487,27 +492,25 @@
         inner = mask_ref[1, t][:, :width]
         return [inner * outside[c] - outer * inside[c] for c in range(3)]
 
-    def middle(x, carry):
+    def middle(x):
         t = (x >= 2).astype(jnp.int32) + (x >= rows + 2).astype(jnp.int32)
         force = forcing(0, x, t, WIDE)
         for c in range(3):
             mid[c, x] = base_ref[c, x] + scale_ref[x] * force[c]
-        return carry
-
-    lax.fori_loop(1, rows + 3, middle, 0)
-
-    def flows(x, carry):
+
+    rows_loop(1, rows + 3, 3, middle)
+
+    def flows(x):
         for q, load in enumerate(
             (lambda c: parts[3 + c, x], lambda c: parts[9 + c, x], lambda c: mid[c, x])
         ):
             moved = east_flow([load(c) for c in range(3)], coef, x)
             for i in range(3):
                 flow[3 * q + i, x] = moved[i]
-        return carry
-
-    lax.fori_loop(1, rows + 3, flows, 0)
-
-    def last(x, carry):
+
+    rows_loop(1, rows + 3, 6, flows)
+
+    def last(x):
         force = forcing(1, x, 1, LANE)
         applied = apply_row(lambda c, r: mid[c, r], lambda i, r: flow[6 + i, r], coef, x, LANE)
         scale = scale_ref[x, :, :LANE]
@@ -518,13 +521,12 @@
             next_out[pl.ds(c * lev * rows + x - 2, lev, stride=rows), :] = (
                 2.0 * current - now + scale * (applied[c] + force[c])
             )
-        return carry
-
-    lax.fori_loop(2, rows + 2, last, 0)
+
+    rows_loop(2, rows + 2, 4, last)
 
 
 def specs(text):
-    space = {"v": VMEM, "s": SMEM}
+    space = {"v": VMEM, "s": SMEM, "h": pltpu.HBM}
     return [pl.BlockSpec(memory_space=space[kind]) for kind in text]
 
 
@@ -550,31 +552,48 @@
     assert (c_east, c_north) == (8, 26) and 6 * (rows + 4) <= LANE
     now, prev, dens, mods = (a.reshape(-1, north_cells) for a in (disp_now, disp_prev, density, moduli))
     wide = rows + 4
+    shifts = offsets.transpose(0, 3, 1, 2)
+    limit = pltpu.CompilerParams(vmem_limit_bytes=16 * 2**20)
+    assert n_x % 2 == 0
 
     payload, first, last = pl.pallas_call(
         functools.partial(pre_kernel, lev, rows, groups, samples),
-        out_shape=(f32(n_x * n_y, 40, LANE), f32(15, lev, LANE), f32(15, lev, LANE)),
-        in_specs=specs("vvvvvss"),
+        out_shape=(f32(40, LANE), f32(15, lev, LANE), f32(15, lev, LANE)),
+        in_specs=specs("hhhhhss"),
         out_specs=specs("vvv"),
-        scratch_shapes=[VMEM((24, WIDE), jnp.float32)],
+        scratch_shapes=[VMEM((24, WIDE), jnp.float32)]
+        + [VMEM(a.shape, jnp.float32) for a in (coarse, now, prev, dens, mods)]
+        + [pltpu.SemaphoreType.DMA((5,))],
+        compiler_params=limit,
         name="pre",
-    )(coarse, now, prev, dens, mods, offsets, ranges)
-    got = lax.all_to_all(payload, ("gx", "gy"), split_axis=0, concat_axis=0, tiled=True)
+    )(*(pltpu.with_memory_space_constraint(a, pltpu.HBM) for a in (coarse, now, prev, dens, mods, shifts, ranges)))
+    half = n_x * n_y // 2
+    twin = lax.ppermute(payload, "gx", [(i, (i + n_x // 2) % n_x) for i in range(n_x)])
     before = lax.ppermute(last, "gx", neighbours("gx", 1))
     after = lax.ppermute(first, "gx", neighbours("gx", -1))
+    chunk = jnp.concatenate([payload, twin], axis=0)
+    got = lax.all_to_all(
+        jnp.broadcast_to(chunk[None], (half,) + chunk.shape),
+        ("gx", "gy"),
+        split_axis=0,
+        concat_axis=0,
+        tiled=True,
+        axis_index_groups=[list(range(half)), list(range(half, 2 * half))],
+    ).reshape(2 * half, 40, LANE)
     to_west, to_east, meta = pl.pallas_call(
         functools.partial(pack_kernel, lev, rows, groups),
         out_shape=(f32(4, lev, LANE), f32(4, lev, LANE), f32(lev, LANE)),
         in_specs=specs("vvvvvvss"),
         out_specs=specs("vvv"),
         cost_estimate=pl.CostEstimate(flops=2000000, bytes_accessed=1000000, transcendentals=0),
+        compiler_params=limit,
         name="pack",
-    )(now, prev, dens, mods, before, after, offsets, ranges)
+    )(now, prev, dens, mods, before, after, shifts, ranges)
     west = lax.ppermute(to_east, "gy", neighbours("gy", 1))
     east = lax.ppermute(to_west, "gy", neighbours("gy", -1))
-    place = jnp.stack([lax.axis_index("gx"), lax.axis_index("gy"), jnp.int32(n_y)]).astype(jnp.int32)
+    place = jnp.stack([lax.axis_index("gx"), lax.axis_index("gy")]).astype(jnp.int32)
     prepared = pl.pallas_call(
-        functools.partial(prep_kernel, lev, rows, groups, c_north),
+        functools.partial(prep_kernel, lev, rows, groups, c_north, n_x, n_y),
         out_shape=(
             f32(2, wide, lev, WIDE),
             f32(3, wide, lev, WIDE),
@@ -594,11 +613,12 @@
             VMEM((COEFS, wide, lev, WIDE), jnp.float32),
         ],
         cost_estimate=pl.CostEstimate(flops=10000000, bytes_accessed=3000000, transcendentals=0),
+        compiler_params=limit,
         name="prep",
     )(now, prev, dens, mods, before, after, west, east, meta, block_route, place)
     mods_x, base, scale, mask, level_w, shift, own_hat, side_hat, index = prepared
     incident, mid, nxt = pl.pallas_call(
-        functools.partial(finish_kernel, lev, rows, groups, c_east, c_north, block_hold),
+        functools.partial(finish_kernel, lev, rows, groups, c_east, c_north),
         out_shape=(
             f32(6 * lev * rows, LANE),
             f32(3 * lev * rows, LANE),
@@ -617,6 +637,7 @@
             VMEM((COEFS, wide, lev, WIDE), jnp.float32),
         ],
         cost_estimate=pl.CostEstimate(flops=20000000, bytes_accessed=6000000, transcendentals=0),
+        compiler_params=limit,
         name="finish",
     )(got, index, mods_x, base, scale, mask, level_w, shift, own_hat, side_hat, now)
     return (

time: 65.4 us -> 49.6 us (0.76)
  Pallas kernels: 27.6 us -> 16.4 us
  local copies, waits for them, and re-layouts: 4.03 us -> 0.92 us
  waiting for transfers between devices: 14.3 us -> 12.2 us
  starting transfers between devices: 17.8 us -> 18.9 us
    ppermute x1, waiting for transfers between devices: 11.5 us -> 0.97 us  [local(): before = lax.ppermute(last, 'gx', neighbours('gx', 1))]
    pallas_call x1, Pallas kernels: 14.7 us -> 8.21 us  [local(): pl.pallas_call(functools.partial(finish_kernel, lev, rows, groups, c_east...]
    ppermute x1, waiting for transfers between devices: 0.01 us -> 4.7 us  [local(): after = lax.ppermute(first, 'gx', neighbours('gx', -1))]
    unnamed x15 -> x14, local copies, waits for them, and re-layouts: 4.03 us -> 0.03 us
    ppermute x0 -> x1, waiting for transfers between devices: none -> 3.52 us  [local(): lax.ppermute(payload, 'gx', [(i, (i + n_x // 2) % n_x) for i in range(n_x)])]
    pallas_call x1, Pallas kernels: 8.41 us -> 5.23 us  [local(): pl.pallas_call(functools.partial(prep_kernel, lev, rows, groups, c_north,...]
    pallas_call x1, Pallas kernels: 2.19 us -> 1.01 us  [local(): pl.pallas_call(functools.partial(pack_kernel, lev, rows, groups), out_sha...]
    broadcast_in_dim x0 -> x1, local copies, waits for them, and re-layouts: none -> 0.89 us  [local(): jnp.broadcast_to(chunk[None], (half,) + chunk.shape)]
  transfers between devices with their start and end apart: 5 -> 6, of which waited for: 2 -> 4; matrix products, arithmetic and copies ran while one was open for 1% -> 0% of each run, Pallas kernels for 16% -> 13%
where the time goes in v2:
time: 49.6 us; the launch traced here: 49.3 us
  starting transfers between devices  18.9 us (38%)
  Pallas kernels  16.4 us (33%)
  waiting for transfers between devices  12.2 us (25%)
  local copies, waits for them, and re-layouts  0.92 us (2%)
  between operations  0.76 us (2%)
    pallas_call x1, Pallas kernels, local(): pl.pallas_call(functools.partial(finish_kernel, lev, rows, groups, c_east...  8.21 us
    all_to_all x1, starting transfers between devices, local(): lax.all_to_all(jnp.broadcast_to(chunk[None], (half,) + chunk.shape), ('gx...  6.82 us
    pallas_call x1, Pallas kernels, local(): pl.pallas_call(functools.partial(prep_kernel, lev, rows, groups, c_north,...  5.23 us
    ppermute x1, waiting for transfers between devices, local(): after = lax.ppermute(first, 'gx', neighbours('gx', -1))  4.7 us
    ppermute x1, starting transfers between devices, local(): west = lax.ppermute(to_east, 'gy', neighbours('gy', 1))  3.95 us
    ppermute x1, waiting for transfers between devices, local(): lax.ppermute(payload, 'gx', [(i, (i + n_x // 2) % n_x) for i in range(n_x)])  3.52 us
    ppermute x1, starting transfers between devices, local(): before = lax.ppermute(last, 'gx', neighbours('gx', 1))  3.25 us
    ppermute x1, waiting for transfers between devices, local(): east = lax.ppermute(to_west, 'gy', neighbours('gy', -1))  3.05 us
  transfers between devices with their start and end apart: 6, of which 4 were waited for; matrix products, arithmetic and copies ran while one was open for 0% of the time, Pallas kernels for 13%

profile of v2, /device:TPU:17, one launch (start us, length us, event | category | flops | bytes accessed | tf_op | source)
XLA Modules:
  0.0 49.3 jit_solution(12646862484969340542)
XLA Ops:
  0.6 1.9 %pre.1 = (f32[40,128]{1,0:T(8,128)S(1)}, f32[15,8,128]{2,1,0:T(8,128)S(1)}, f32[15,8,128]{2,1,0:T(8,128)S(1)}) custom-call(f32[2,24,256]{2,1,0:T(8,128)} %refs_0_.1, f32[384,128]{1,0:T(8,128)} %bitcast.11, f32[384,128]{1,0:T(8,128)} %bitcast.16, f32[128,128]{1,0:T(8,128)} %bitcast.22, f32[256,128]{1,0:T(8,128)} %bitcast.19, s32[1,3,1,4]{3,2,1,0:T(1,128)} %bitcast.25, ...), custom_call_target="tpu_custom_call" | custom-call | tf_op jit(solution)/shard_map/pre/pallas_call | solution.py:559
  2.6 0.1 collective-permute-start
  2.6 3.5 %collective-permute-done = f32[40,128]{1,0:T(8,128)S(1)} collective-permute-done((f32[40,128]{1,0:T(8,128)S(1)}, f32[40,128]{1,0:T(8,128)S(1)}, u32[]{:S(2)}, u32[]{:S(2)}) %collective-permute-start) | collective-permute-done | bytes 20512 | tf_op jit(solution)/shard_map/ppermute | solution.py:571
  6.2 0.9 %broadcast_in_dim.2 = f32[16,80,128]{2,1,0:T(8,128)} broadcast(f32[80,128]{1,0:T(8,128)S(1)} %pad_maximum_fusion), dimensions={1,2} | broadcast | bytes 696320 | tf_op jit(solution)/shard_map/broadcast_in_dim | solution.py:576
  7.1 0.0 copy-start
  7.1 0.0 copy-start.1
  7.1 0.0 copy-start.2
  7.1 0.0 copy-start.3
  7.1 6.8 %all-to-all-start = ((f32[16,80,128]{2,1,0:T(8,128)}), f32[16,80,128]{2,1,0:T(8,128)S(1)}, u32[]{:S(2)}, u32[]{:S(2)}) async-start(f32[16,80,128]{2,1,0:T(8,128)} %broadcast_in_dim.2), calls=%async_computation | async-start | bytes 1310720 | tf_op jit(solution)/shard_map/all_to_all | solution.py:575
  13.9 3.2 %collective-permute-start.1 = (f32[15,8,128]{2,1,0:T(8,128)S(1)}, f32[15,8,128]{2,1,0:T(8,128)S(1)}, u32[]{:S(2)}, u32[]{:S(2)}) collective-permute-start(f32[15,8,128]{2,1,0:T(8,128)S(1)} %get-tuple-element.22), channel_id=1, source_target_pairs={{0,4},{4,8},{8,12},{12,16},{16,20},{20,24},{24,28},{1,5},{5,9},{9,... | collective-permute-start | bytes 184328 | tf_op jit(solution)/shard_map/ppermute | solution.py:572
  17.1 2.9 %collective-permute-start.2 = (f32[15,8,128]{2,1,0:T(8,128)S(1)}, f32[15,8,128]{2,1,0:T(8,128)S(1)}, u32[]{:S(2)}, u32[]{:S(2)}) collective-permute-start(f32[15,8,128]{2,1,0:T(8,128)S(1)} %get-tuple-element.23), channel_id=1, source_target_pairs={{4,0},{8,4},{12,8},{16,12},{20,16},{24,20},{28,24},{5,1},{9,5},{13... | collective-permute-start | bytes 184328 | tf_op jit(solution)/shard_map/ppermute | solution.py:573
  20.1 0.0 copy-start.4
  20.1 0.0 copy-start.5
  20.1 1.0 %collective-permute-done.1.before_ref = f32[15,8,128]{2,1,0:T(8,128)S(1)} collective-permute-done((f32[15,8,128]{2,1,0:T(8,128)S(1)}, f32[15,8,128]{2,1,0:T(8,128)S(1)}, u32[]{:S(2)}, u32[]{:S(2)}) %collective-permute-start.1) | collective-permute-done | bytes 61472 | tf_op jit(solution)/shard_map/ppermute | solution.py:572
  21.1 4.7 %collective-permute-done.2.after_ref = f32[15,8,128]{2,1,0:T(8,128)S(1)} collective-permute-done((f32[15,8,128]{2,1,0:T(8,128)S(1)}, f32[15,8,128]{2,1,0:T(8,128)S(1)}, u32[]{:S(2)}, u32[]{:S(2)}) %collective-permute-start.2) | collective-permute-done | bytes 61472 | tf_op jit(solution)/shard_map/ppermute | solution.py:573
  25.8 0.0 copy-done
  25.8 0.0 copy-done.1
  25.8 0.0 copy-done.2
  25.8 0.0 copy-done.3
  25.8 0.0 copy-done.4
  25.8 0.0 copy-done.5
  25.8 1.0 %pack.1 = (f32[4,8,128]{2,1,0:T(8,128)S(1)}, f32[4,8,128]{2,1,0:T(8,128)S(1)}, f32[8,128]{1,0:T(8,128)S(1)}) custom-call(f32[384,128]{1,0:T(8,128)S(1)} %bitcast.12, f32[384,128]{1,0:T(8,128)S(1)} %bitcast.17, f32[128,128]{1,0:T(8,128)S(1)} %bitcast.23, f32[256,128]{1,0:T(8,128)S(1)} %bitcast.20, f32[15,8,128]{2,1,0:T(8,128)S(1)} %collective-permute-done.1.before_ref, ...), custom_call_target="tpu_custom_call" | custom-call | flops 2000000 | bytes 1000000 | tf_op jit(solution)/shard_map/pack/pallas_call | solution.py:583
  26.8 3.9 %collective-permute-start.3 = (f32[4,8,128]{2,1,0:T(8,128)S(1)}, f32[4,8,128]{2,1,0:T(8,128)S(1)}, u32[]{:S(2)}, u32[]{:S(2)}) collective-permute-start(f32[4,8,128]{2,1,0:T(8,128)S(1)} %get-tuple-element.24), channel_id=1, source_target_pairs={{0,1},{1,2},{2,3},{4,5},{5,6},{6,7},{8,9},{9,10},{10,11},{12,13},{... | collective-permute-start | bytes 49160 | tf_op jit(solution)/shard_map/ppermute | solution.py:592
  30.8 1.9 %collective-permute-start.4 = (f32[4,8,128]{2,1,0:T(8,128)S(1)}, f32[4,8,128]{2,1,0:T(8,128)S(1)}, u32[]{:S(2)}, u32[]{:S(2)}) collective-permute-start(f32[4,8,128]{2,1,0:T(8,128)S(1)} %get-tuple-element.25), channel_id=1, source_target_pairs={{1,0},{2,1},{3,2},{5,4},{6,5},{7,6},{9,8},{10,9},{11,10},{13,12},{... | collective-permute-start | bytes 49160 | tf_op jit(solution)/shard_map/ppermute | solution.py:593
  32.7 0.1 pad_add_fusion.place_ref
  32.8 0.0 copy-start.6
  32.8 0.0 collective-permute-done.3.west_ref
  32.8 3.0 %collective-permute-done.4.east_ref = f32[4,8,128]{2,1,0:T(8,128)S(1)} collective-permute-done((f32[4,8,128]{2,1,0:T(8,128)S(1)}, f32[4,8,128]{2,1,0:T(8,128)S(1)}, u32[]{:S(2)}, u32[]{:S(2)}) %collective-permute-start.4) | collective-permute-done | bytes 16416 | tf_op jit(solution)/shard_map/ppermute | solution.py:593
  35.8 0.0 copy-done.6
  35.8 5.2 %prep.1 = (f32[2,20,8,256]{3,2,1,0:T(8,128)S(1)}, f32[3,20,8,256]{3,2,1,0:T(8,128)S(1)}, f32[20,8,256]{2,1,0:T(8,128)S(1)}, f32[2,3,8,256]{3,2,1,0:T(8,128)S(1)}...) custom-call(f32[384,128]{1,0:T(8,128)S(1)} %bitcast.13, ...), custom_call_target="tpu_custom_call" | custom-call | flops 10000000 | bytes 3000000 | tf_op jit(solution)/shard_map/prep/pallas_call | solution.py:595
  41.1 0.0 all-to-all-done
  41.1 8.2 %finish.1 = (f32[768,128]{1,0:T(8,128)}, f32[384,128]{1,0:T(8,128)}, f32[384,128]{1,0:T(8,128)}) custom-call(f32[32,40,128]{2,1,0:T(8,128)S(1)} %bitcast.15, s32[36]{0:T(128)S(1)} %get-tuple-element.27.index_ref, f32[2,20,8,256]{3,2,1,0:T(8,128)S(1)} %get-tuple-element.28.mods_ref, f32[3,20,8,256]{3,2,1,0:T(8,128)S(1)} %get-tuple-element.29.base_ref, ...), custom_call_target="tpu_custom_call" | custom-call | flops 20000000 | bytes 6000000 | tf_op jit(solution)/shard_map/finish/pallas_call | solution.py:620
  (1 shorter events, 0.0 us)
Async XLA Ops:
  2.6 3.6 %collective-permute-start = (f32[40,128]{1,0:T(8,128)S(1)}, f32[40,128]{1,0:T(8,128)S(1)}, u32[]{:S(2)}, u32[]{:S(2)}) collective-permute-start(f32[40,128]{1,0:T(8,128)S(1)} %get-tuple-element.21), channel_id=1, source_target_pairs={{0,16},{4,20},{8,24},{12,28},{16,0},{20,4},{24,8},{28,12},{1,17},{... | collective-permute-start | bytes 61448 | tf_op jit(solution)/shard_map/ppermute | solution.py:571
  7.1 18.7 %copy-start = (f32[3,8,16,128]{3,2,1,0:T(8,128)S(1)}, f32[3,8,16,128]{3,2,1,0:T(8,128)}, u32[]{:S(2)}) copy-start(f32[3,8,16,128]{3,2,1,0:T(8,128)} %param.8) | copy-start | bytes 589828
  7.1 18.7 %copy-start.1 = (f32[3,8,16,128]{3,2,1,0:T(8,128)S(1)}, f32[3,8,16,128]{3,2,1,0:T(8,128)}, u32[]{:S(2)}) copy-start(f32[3,8,16,128]{3,2,1,0:T(8,128)} %param.9) | copy-start | bytes 589828
  7.1 18.7 %copy-start.2 = (f32[2,8,16,128]{3,2,1,0:T(8,128)S(1)}, f32[2,8,16,128]{3,2,1,0:T(8,128)}, u32[]{:S(2)}) copy-start(f32[2,8,16,128]{3,2,1,0:T(8,128)} %param.11) | copy-start | bytes 393220
  7.1 18.7 %copy-start.3 = (f32[8,16,128]{2,1,0:T(8,128)S(1)}, f32[8,16,128]{2,1,0:T(8,128)}, u32[]{:S(2)}) copy-start(f32[8,16,128]{2,1,0:T(8,128)} %param.10) | copy-start | bytes 196612
  7.1 34.0 %all-to-all-start = ((f32[16,80,128]{2,1,0:T(8,128)}), f32[16,80,128]{2,1,0:T(8,128)S(1)}, u32[]{:S(2)}, u32[]{:S(2)}) async-start(f32[16,80,128]{2,1,0:T(8,128)} %broadcast_in_dim.2), calls=%async_computation | async-start | bytes 1310720 | tf_op jit(solution)/shard_map/all_to_all | solution.py:575
  13.9 7.2 %collective-permute-start.1 = (f32[15,8,128]{2,1,0:T(8,128)S(1)}, f32[15,8,128]{2,1,0:T(8,128)S(1)}, u32[]{:S(2)}, u32[]{:S(2)}) collective-permute-start(f32[15,8,128]{2,1,0:T(8,128)S(1)} %get-tuple-element.22), channel_id=1, source_target_pairs={{0,4},{4,8},{8,12},{12,16},{16,20},{20,24},{24,28},{1,5},{5,9},{9,... | collective-permute-start | bytes 184328 | tf_op jit(solution)/shard_map/ppermute | solution.py:572
  17.1 8.6 %collective-permute-start.2 = (f32[15,8,128]{2,1,0:T(8,128)S(1)}, f32[15,8,128]{2,1,0:T(8,128)S(1)}, u32[]{:S(2)}, u32[]{:S(2)}) collective-permute-start(f32[15,8,128]{2,1,0:T(8,128)S(1)} %get-tuple-element.23), channel_id=1, source_target_pairs={{4,0},{8,4},{12,8},{16,12},{20,16},{24,20},{28,24},{5,1},{9,5},{13... | collective-permute-start | bytes 184328 | tf_op jit(solution)/shard_map/ppermute | solution.py:573
  20.1 5.7 %copy-start.4 = (s32[1,1,4,3]{2,1,3,0:T(1,128)S(1)}, s32[1,1,4,3]{2,1,3,0:T(1,128)}, u32[]{:S(2)}) copy-start(s32[1,1,4,3]{2,1,3,0:T(1,128)} %param.15) | copy-start | bytes 148
  20.1 5.7 %copy-start.5 = (s32[1,1,2]{2,1,0:T(1,128)S(1)}, s32[1,1,2]{2,1,0:T(1,128)}, u32[]{:S(2)}) copy-start(s32[1,1,2]{2,1,0:T(1,128)} %rng_ref.1) | copy-start | bytes 28
  26.8 6.0 %collective-permute-start.3 = (f32[4,8,128]{2,1,0:T(8,128)S(1)}, f32[4,8,128]{2,1,0:T(8,128)S(1)}, u32[]{:S(2)}, u32[]{:S(2)}) collective-permute-start(f32[4,8,128]{2,1,0:T(8,128)S(1)} %get-tuple-element.24), channel_id=1, source_target_pairs={{0,1},{1,2},{2,3},{4,5},{5,6},{6,7},{8,9},{9,10},{10,11},{12,13},{... | collective-permute-start | bytes 49160 | tf_op jit(solution)/shard_map/ppermute | solution.py:592
  30.8 5.1 %collective-permute-start.4 = (f32[4,8,128]{2,1,0:T(8,128)S(1)}, f32[4,8,128]{2,1,0:T(8,128)S(1)}, u32[]{:S(2)}, u32[]{:S(2)}) collective-permute-start(f32[4,8,128]{2,1,0:T(8,128)S(1)} %get-tuple-element.25), channel_id=1, source_target_pairs={{1,0},{2,1},{3,2},{5,4},{6,5},{7,6},{9,8},{10,9},{11,10},{13,12},{... | collective-permute-start | bytes 49160 | tf_op jit(solution)/shard_map/ppermute | solution.py:593
  32.8 3.1 %copy-start.6 = (s32[64]{0:T(128)S(1)}, s32[64]{0:T(128)}, u32[]{:S(2)}) copy-start(s32[64]{0:T(128)} %route_ref.1) | copy-start | bytes 772

commit v3 on v2

--- a/solution.py
+++ b/solution.py
@@ -55,6 +55,10 @@
         return carry
 
     lax.fori_loop(0, (stop - start) // step, chunk, 0)
+
+
+def quotient(v, n):
+    return v >> (n.bit_length() - 1) if n & (n - 1) == 0 else lax.div(v, n)
 
 
 def meta_vector(off_ref, rng_ref, groups):
@@ -134,7 +138,7 @@
 
 
 def pack_kernel(
-    lev, rows, groups, now_ref, prev_ref, dens_ref, mod_ref, before_ref, after_ref, off_ref, rng_ref,
+    lev, rows, now_ref, prev_ref, dens_ref, mod_ref, before_ref, after_ref, own_ref,
     west_ref, east_ref, meta_ref
 ):
     refs = (now_ref, prev_ref, dens_ref, mod_ref, before_ref, after_ref)
@@ -155,8 +159,7 @@
         west_ref[block] = west
         east_ref[block] = east
     sub = sub_ids((lev, LANE))
-    meta = meta_vector(off_ref, rng_ref, groups)
-    both = jnp.where(sub == 0, before_ref[14], jnp.where(sub == 1, meta, after_ref[14]))
+    both = jnp.where(sub == 0, before_ref[14], jnp.where(sub == 1, own_ref[14], after_ref[14]))
     west_ref[3] = both
     east_ref[3] = both
     meta_ref[...] = both
@@ -245,42 +248,41 @@
     return out
 
 
+def index_kernel(groups, n_x, n_y, route_ref, place_ref, index_ref):
+    my_x, my_y = place_ref[0], place_ref[1]
+    for i in range(9 * groups):
+        index_ref[i] = 0
+    half = n_x * n_y // 2
+    upper = (2 * my_x >= n_x).astype(jnp.int32)
+
+    def find(b):
+        slot = route_ref[b]
+        tile = quotient(slot, groups)
+        tile_x = quotient(tile, n_y)
+        d_x = tile_x - my_x + 1
+        d_y = tile - tile_x * n_y - my_y
+        column = jnp.where(d_y < 0, 2, d_y)
+        near = (d_x >= 0) & (d_x < 3) & (d_y >= -1) & (d_y < 2)
+        at = jnp.where(near, (d_x * 3 + column) * groups + slot - tile * groups, 9 * groups)
+        source = quotient(b, 2)
+        far = (source >= half).astype(jnp.int32)
+        seat = 2 * (source - far * half) + (far ^ upper)
+        index_ref[at] = 2 * seat + b - 2 * source
+
+    rows_loop(0, route_ref.shape[0], 16, find)
+
+
 def prep_kernel(
-    lev, rows, groups, c_north, n_x, n_y, now_ref, prev_ref, dens_ref, mod_ref, before_ref, after_ref, west_ref, east_ref, meta_ref,
-    route_ref, place_ref, mods_ref, base_ref, scale_ref, mask_ref, level_ref, shift_ref, own_hat_ref, side_hat_ref,
-    index_ref, now_x, flow, coef
+    lev, rows, groups, c_north, now_ref, prev_ref, dens_ref, mod_ref, before_ref, after_ref, west_ref, east_ref, meta_ref,
+    mods_ref, base_ref, scale_ref, mask_ref, level_ref, shift_ref, own_hat_ref, side_hat_ref,
+    now_x, flow, coef
 ):
     refs = (now_ref, prev_ref, dens_ref, mod_ref, before_ref, after_ref)
     lane = lane_ids((lev, LANE))
     sub = sub_ids((lev, LANE))
     span = 2 * (rows + 4)
+
     metas = (meta_ref[...], east_ref[3], west_ref[3])
-
-    for i in range(9 * groups):
-        index_ref[i] = 0
-    my_x, my_y = place_ref[0], place_ref[1]
-    half = n_x * n_y // 2
-    upper = (2 * my_x >= n_x).astype(jnp.int32)
-
-    def find(b, carry):
-        slot = route_ref[b]
-        tile = lax.div(slot, groups)
-        g = slot - tile * groups
-        tile_x = lax.div(tile, n_y)
-        d_x = tile_x - my_x + 1
-        d_y = tile - tile_x * n_y - my_y
-        column = jnp.where(d_y < 0, 2, d_y)
-
-        @pl.when((d_x >= 0) & (d_x < 3) & (d_y >= -1) & (d_y < 2))
-        def _():
-            source = lax.div(b, 2)
-            far = (source >= half).astype(jnp.int32)
-            seat = 2 * (source - far * half) + (far ^ upper)
-            index_ref[(d_x * 3 + column) * groups + g] = 2 * seat + b - 2 * source
-
-        return carry
-
-    lax.fori_loop(0, route_ref.shape[0], find, 0)
 
     def sides(plane, x):
         block, p = divmod(plane, 3)
@@ -312,7 +314,7 @@
         for i in range(3):
             flow[i, x] = parts[i]
 
-    rows_loop(0, rows + 4, 5, first)
+    rows_loop(0, rows + 4, 10, first)
     rows_loop(1, rows + 3, 6, lambda x: coef_row(mods_ref, coef, x))
 
     def second(x):
@@ -320,7 +322,7 @@
         for c in range(3):
             base_ref[c, x] = 2.0 * now_x[c, x] - base_ref[c, x] + scale_ref[x] * applied[c]
 
-    rows_loop(1, rows + 3, 3, second)
+    rows_loop(1, rows + 3, 9, second)
 
     group_of_sub = sub // 2
     second_level = (sub - 2 * group_of_sub).astype(jnp.float32)
@@ -471,22 +473,23 @@
             parts[6 + nc, x] = inner * total
             if not isinstance(cell, int):
                 inc_out[pl.ds(nc * lev * rows + cell, lev, stride=rows), :] = total[:, :LANE]
-        for q, mask in enumerate((outer, inner)):
-            moved = east_flow([mask * values[c] for c in range(3)], coef, x)
-            for i in range(3):
-                flow[3 * q + i, x] = moved[i]
-
-    rows_loop(0, rows, 4, lambda cell: east(cell + 2, 1, cell))
+        for n in range(2):
+            for q, mask in enumerate((outer, inner)):
+                moved = east_flow([mask * values[3 * n + c] for c in range(3)], coef, x)
+                for i in range(3):
+                    flow[6 * n + 3 * q + i, x] = moved[i]
+
+    rows_loop(0, rows, 8, lambda cell: east(cell + 2, 1, cell))
     for r in range(2):
         east(r, 0, rows - 2 + r)
         east(rows + 2 + r, 2, r)
 
     def forcing(step, x, t, width):
         outside = apply_row(
-            lambda c, r: parts[3 * step + c, r], lambda i, r: flow[i, r], coef, x, width
+            lambda c, r: parts[3 * step + c, r], lambda i, r: flow[6 * step + i, r], coef, x, width
         )
         inside = apply_row(
-            lambda c, r: parts[6 + 3 * step + c, r], lambda i, r: flow[3 + i, r], coef, x, width
+            lambda c, r: parts[6 + 3 * step + c, r], lambda i, r: flow[6 * step + 3 + i, r], coef, x, width
         )
         outer = mask_ref[0, t][:, :width]
         inner = mask_ref[1, t][:, :width]
@@ -498,21 +501,18 @@
         for c in range(3):
             mid[c, x] = base_ref[c, x] + scale_ref[x] * force[c]
 
-    rows_loop(1, rows + 3, 3, middle)
+    rows_loop(1, rows + 3, 9, middle)
 
     def flows(x):
-        for q, load in enumerate(
-            (lambda c: parts[3 + c, x], lambda c: parts[9 + c, x], lambda c: mid[c, x])
-        ):
-            moved = east_flow([load(c) for c in range(3)], coef, x)
-            for i in range(3):
-                flow[3 * q + i, x] = moved[i]
-
-    rows_loop(1, rows + 3, 6, flows)
+        moved = east_flow([mid[c, x] for c in range(3)], coef, x)
+        for i in range(3):
+            flow[12 + i, x] = moved[i]
+
+    rows_loop(1, rows + 3, 18, flows)
 
     def last(x):
         force = forcing(1, x, 1, LANE)
-        applied = apply_row(lambda c, r: mid[c, r], lambda i, r: flow[6 + i, r], coef, x, LANE)
+        applied = apply_row(lambda c, r: mid[c, r], lambda i, r: flow[12 + i, r], coef, x, LANE)
         scale = scale_ref[x, :, :LANE]
         for c in range(3):
             now = now_ref[pl.ds(c * lev * rows + x - 2, lev, stride=rows), :]
@@ -522,7 +522,7 @@
                 2.0 * current - now + scale * (applied[c] + force[c])
             )
 
-    rows_loop(2, rows + 2, 4, last)
+    rows_loop(2, rows + 2, 16, last)
 
 
 def specs(text):
@@ -581,19 +581,28 @@
         axis_index_groups=[list(range(half)), list(range(half, 2 * half))],
     ).reshape(2 * half, 40, LANE)
     to_west, to_east, meta = pl.pallas_call(
-        functools.partial(pack_kernel, lev, rows, groups),
+        functools.partial(pack_kernel, lev, rows),
         out_shape=(f32(4, lev, LANE), f32(4, lev, LANE), f32(lev, LANE)),
-        in_specs=specs("vvvvvvss"),
+        in_specs=specs("vvvvvvv"),
         out_specs=specs("vvv"),
         cost_estimate=pl.CostEstimate(flops=2000000, bytes_accessed=1000000, transcendentals=0),
         compiler_params=limit,
         name="pack",
-    )(now, prev, dens, mods, before, after, shifts, ranges)
+    )(now, prev, dens, mods, before, after, first)
     west = lax.ppermute(to_east, "gy", neighbours("gy", 1))
     east = lax.ppermute(to_west, "gy", neighbours("gy", -1))
     place = jnp.stack([lax.axis_index("gx"), lax.axis_index("gy")]).astype(jnp.int32)
+    index = pl.pallas_call(
+        functools.partial(index_kernel, groups, n_x, n_y),
+        out_shape=jax.ShapeDtypeStruct((9 * groups + 1,), jnp.int32),
+        in_specs=specs("ss"),
+        out_specs=specs("s")[0],
+        compiler_params=limit,
+        cost_estimate=pl.CostEstimate(flops=2000000, bytes_accessed=1000, transcendentals=0),
+        name="index",
+    )(block_route, place)
     prepared = pl.pallas_call(
-        functools.partial(prep_kernel, lev, rows, groups, c_north, n_x, n_y),
+        functools.partial(prep_kernel, lev, rows, groups, c_north),
         out_shape=(
             f32(2, wide, lev, WIDE),
             f32(3, wide, lev, WIDE),
@@ -603,10 +612,9 @@
             f32(3, lev, WIDE),
             jax.ShapeDtypeStruct((3, LANE, LANE), jnp.bfloat16),
             jax.ShapeDtypeStruct((3, WIDE, LANE), jnp.bfloat16),
-            jax.ShapeDtypeStruct((9 * groups,), jnp.int32),
         ),
-        in_specs=specs("vvvvvvvvvss"),
-        out_specs=specs("vvvvvvvvs"),
+        in_specs=specs("v" * 9),
+        out_specs=specs("v" * 8),
         scratch_shapes=[
             VMEM((3, wide, lev, WIDE), jnp.float32),
             VMEM((3, wide, lev, WIDE), jnp.float32),
@@ -615,8 +623,8 @@
         cost_estimate=pl.CostEstimate(flops=10000000, bytes_accessed=3000000, transcendentals=0),
         compiler_params=limit,
         name="prep",
-    )(now, prev, dens, mods, before, after, west, east, meta, block_route, place)
-    mods_x, base, scale, mask, level_w, shift, own_hat, side_hat, index = prepared
+    )(now, prev, dens, mods, before, after, west, east, meta)
+    mods_x, base, scale, mask, level_w, shift, own_hat, side_hat = prepared
     incident, mid, nxt = pl.pallas_call(
         functools.partial(finish_kernel, lev, rows, groups, c_east, c_north),
         out_shape=(
@@ -632,7 +640,7 @@
             VMEM((6 * c_east * lev, WIDE), jnp.float32),
             VMEM((3, 6 * c_east, lev, WIDE), jnp.float32),
             VMEM((12, wide, lev, WIDE), jnp.float32),
-            VMEM((9, wide, lev, WIDE), jnp.float32),
+            VMEM((15, wide, lev, WIDE), jnp.float32),
             VMEM((3, wide, lev, WIDE), jnp.float32),
             VMEM((COEFS, wide, lev, WIDE), jnp.float32),
         ],

time: 49.6 us -> 45 us (0.907)
  Pallas kernels: 16.4 us -> 13.8 us
  waiting for transfers between devices: 12.2 us -> 9.65 us
  local copies, waits for them, and re-layouts: 0.92 us -> 1.48 us
    ppermute x1, waiting for transfers between devices: 3.05 us -> 0.43 us  [local(): east = lax.ppermute(to_west, 'gy', neighbours('gy', -1))]
    pallas_call x2 -> x3, Pallas kernels: 6.24 us -> 4.67 us  [the longest x1 2.2 us: local(): pl.pallas_call(functools.partial(prep_kernel, lev, rows, groups, c_north)...]
    pallas_call x1, Pallas kernels: 8.21 us -> 7.16 us  [local(): pl.pallas_call(functools.partial(finish_kernel, lev, rows, groups, c_east...]
    unnamed x14 -> x10, local copies, waits for them, and re-layouts: 0.03 us -> 0.59 us
  transfers between devices with their start and end apart: 6 -> 6, of which waited for: 4 -> 4; matrix products, arithmetic and copies ran while one was open for 0% -> 0% of each run, Pallas kernels for 13% -> 10%
where the time goes in v3:
time: 45 us; the launch traced here: 44.6 us
  starting transfers between devices  18.9 us (42%)
  Pallas kernels  13.8 us (31%)
  waiting for transfers between devices  9.65 us (21%)
  local copies, waits for them, and re-layouts  1.48 us (3%)
  between operations  0.75 us (2%)
    pallas_call x1, Pallas kernels, local(): pl.pallas_call(functools.partial(finish_kernel, lev, rows, groups, c_east...  7.16 us
    all_to_all x1, starting transfers between devices, local(): lax.all_to_all(jnp.broadcast_to(chunk[None], (half,) + chunk.shape), ('gx...  6.82 us
    ppermute x1, waiting for transfers between devices, local(): after = lax.ppermute(first, 'gx', neighbours('gx', -1))  4.7 us
    ppermute x1, starting transfers between devices, local(): west = lax.ppermute(to_east, 'gy', neighbours('gy', 1))  3.95 us
    ppermute x1, waiting for transfers between devices, local(): lax.ppermute(payload, 'gx', [(i, (i + n_x // 2) % n_x) for i in range(n_x)])  3.52 us
    ppermute x1, starting transfers between devices, local(): before = lax.ppermute(last, 'gx', neighbours('gx', 1))  3.25 us
    ppermute x1, starting transfers between devices, local(): after = lax.ppermute(first, 'gx', neighbours('gx', -1))  2.92 us
    pallas_call x1, Pallas kernels, local(): pl.pallas_call(functools.partial(prep_kernel, lev, rows, groups, c_north)...  2.2 us
  transfers between devices with their start and end apart: 6, of which 4 were waited for; matrix products, arithmetic and copies ran while one was open for 0% of the time, Pallas kernels for 10%

profile of v3, /device:TPU:17, one launch (start us, length us, event | category | flops | bytes accessed | tf_op | source)
XLA Modules:
  0.0 44.6 jit_solution(15958170490283732068)
XLA Ops:
  0.6 1.9 %pre.1 = (f32[40,128]{1,0:T(8,128)S(1)}, f32[15,8,128]{2,1,0:T(8,128)S(1)}, f32[15,8,128]{2,1,0:T(8,128)S(1)}) custom-call(f32[2,24,256]{2,1,0:T(8,128)} %refs_0_.1, f32[384,128]{1,0:T(8,128)} %bitcast.11, f32[384,128]{1,0:T(8,128)} %bitcast.16, f32[128,128]{1,0:T(8,128)} %bitcast.22, f32[256,128]{1,0:T(8,128)} %bitcast.19, s32[1,3,1,4]{3,2,1,0:T(1,128)} %bitcast.25, ...), custom_call_target="tpu_custom_call" | custom-call | tf_op jit(solution)/shard_map/pre/pallas_call | solution.py:559
  2.6 0.1 collective-permute-start
  2.6 3.5 %collective-permute-done = f32[40,128]{1,0:T(8,128)S(1)} collective-permute-done((f32[40,128]{1,0:T(8,128)S(1)}, f32[40,128]{1,0:T(8,128)S(1)}, u32[]{:S(2)}, u32[]{:S(2)}) %collective-permute-start) | collective-permute-done | bytes 20512 | tf_op jit(solution)/shard_map/ppermute | solution.py:571
  6.2 0.9 %broadcast_in_dim.2 = f32[16,80,128]{2,1,0:T(8,128)} broadcast(f32[80,128]{1,0:T(8,128)S(1)} %pad_maximum_fusion), dimensions={1,2} | broadcast | bytes 696320 | tf_op jit(solution)/shard_map/broadcast_in_dim | solution.py:576
  7.1 0.0 copy-start
  7.1 0.0 copy-start.1
  7.1 0.0 copy-start.2
  7.1 0.0 copy-start.3
  7.1 6.8 %all-to-all-start = ((f32[16,80,128]{2,1,0:T(8,128)}), f32[16,80,128]{2,1,0:T(8,128)S(1)}, u32[]{:S(2)}, u32[]{:S(2)}) async-start(f32[16,80,128]{2,1,0:T(8,128)} %broadcast_in_dim.2), calls=%async_computation | async-start | bytes 1310720 | tf_op jit(solution)/shard_map/all_to_all | solution.py:575
  13.9 3.2 %collective-permute-start.1 = (f32[15,8,128]{2,1,0:T(8,128)S(1)}, f32[15,8,128]{2,1,0:T(8,128)S(1)}, u32[]{:S(2)}, u32[]{:S(2)}) collective-permute-start(f32[15,8,128]{2,1,0:T(8,128)S(1)} %get-tuple-element.21), channel_id=1, source_target_pairs={{0,4},{4,8},{8,12},{12,16},{16,20},{20,24},{24,28},{1,5},{5,9},{9,... | collective-permute-start | bytes 184328 | tf_op jit(solution)/shard_map/ppermute | solution.py:572
  17.1 2.9 %collective-permute-start.2 = (f32[15,8,128]{2,1,0:T(8,128)S(1)}, f32[15,8,128]{2,1,0:T(8,128)S(1)}, u32[]{:S(2)}, u32[]{:S(2)}) collective-permute-start(f32[15,8,128]{2,1,0:T(8,128)S(1)} %get-tuple-element.22.own_ref), channel_id=1, source_target_pairs={{4,0},{8,4},{12,8},{16,12},{20,16},{24,20},{28,24},{5,1},{9,5},{13... | collective-permute-start | bytes 184328 | tf_op jit(solution)/shard_map/ppermute | solution.py:573
  20.1 1.0 %collective-permute-done.1.before_ref = f32[15,8,128]{2,1,0:T(8,128)S(1)} collective-permute-done((f32[15,8,128]{2,1,0:T(8,128)S(1)}, f32[15,8,128]{2,1,0:T(8,128)S(1)}, u32[]{:S(2)}, u32[]{:S(2)}) %collective-permute-start.1) | collective-permute-done | bytes 61472 | tf_op jit(solution)/shard_map/ppermute | solution.py:572
  21.1 4.7 %collective-permute-done.2.after_ref = f32[15,8,128]{2,1,0:T(8,128)S(1)} collective-permute-done((f32[15,8,128]{2,1,0:T(8,128)S(1)}, f32[15,8,128]{2,1,0:T(8,128)S(1)}, u32[]{:S(2)}, u32[]{:S(2)}) %collective-permute-start.2) | collective-permute-done | bytes 61472 | tf_op jit(solution)/shard_map/ppermute | solution.py:573
  25.8 0.0 copy-done
  25.8 0.0 copy-done.1
  25.8 0.0 copy-done.2
  25.8 0.0 copy-done.3
  25.8 0.4 pack.1
  26.2 3.9 %collective-permute-start.3 = (f32[4,8,128]{2,1,0:T(8,128)S(1)}, f32[4,8,128]{2,1,0:T(8,128)S(1)}, u32[]{:S(2)}, u32[]{:S(2)}) collective-permute-start(f32[4,8,128]{2,1,0:T(8,128)S(1)} %get-tuple-element.23), channel_id=1, source_target_pairs={{0,1},{1,2},{2,3},{4,5},{5,6},{6,7},{8,9},{9,10},{10,11},{12,13},{... | collective-permute-start | bytes 49160 | tf_op jit(solution)/shard_map/ppermute | solution.py:592
  30.2 1.9 %collective-permute-start.4 = (f32[4,8,128]{2,1,0:T(8,128)S(1)}, f32[4,8,128]{2,1,0:T(8,128)S(1)}, u32[]{:S(2)}, u32[]{:S(2)}) collective-permute-start(f32[4,8,128]{2,1,0:T(8,128)S(1)} %get-tuple-element.24), channel_id=1, source_target_pairs={{1,0},{2,1},{3,2},{5,4},{6,5},{7,6},{9,8},{10,9},{11,10},{13,12},{... | collective-permute-start | bytes 49160 | tf_op jit(solution)/shard_map/ppermute | solution.py:593
  32.1 0.0 copy-start.4
  32.1 0.1 pad_add_fusion.place_ref
  32.2 0.6 %copy-done.4 = s32[64]{0:T(128)S(1)} copy-done((s32[64]{0:T(128)S(1)}, s32[64]{0:T(128)}, u32[]{:S(2)}) %copy-start.4) | copy-done | bytes 280
  32.8 2.0 %index.1.index_ref = s32[37]{0:T(128)S(1)} custom-call(s32[64]{0:T(128)S(1)} %copy-done.4, s32[2]{0:T(128)S(1)} %pad_add_fusion.place_ref), custom_call_target="tpu_custom_call" | custom-call | flops 2000000 | bytes 1000 | tf_op jit(solution)/shard_map/index/pallas_call | solution.py:595
  34.8 0.0 collective-permute-done.3.west_ref
  34.8 0.4 collective-permute-done.4.east_ref
  35.3 2.2 %prep.1 = (f32[2,20,8,256]{3,2,1,0:T(8,128)S(1)}, f32[3,20,8,256]{3,2,1,0:T(8,128)S(1)}, f32[20,8,256]{2,1,0:T(8,128)S(1)}, f32[2,3,8,256]{3,2,1,0:T(8,128)S(1)}...) custom-call(f32[384,128]{1,0:T(8,128)S(1)} %bitcast.13, ...), custom_call_target="tpu_custom_call" | custom-call | flops 10000000 | bytes 3000000 | tf_op jit(solution)/shard_map/prep/pallas_call | solution.py:604
  37.5 0.0 all-to-all-done
  37.5 7.2 %finish.1 = (f32[768,128]{1,0:T(8,128)}, f32[384,128]{1,0:T(8,128)}, f32[384,128]{1,0:T(8,128)}) custom-call(f32[32,40,128]{2,1,0:T(8,128)S(1)} %bitcast.15, s32[37]{0:T(128)S(1)} %index.1.index_ref, f32[2,20,8,256]{3,2,1,0:T(8,128)S(1)} %get-tuple-element.26.mods_ref, f32[3,20,8,256]{3,2,1,0:T(8,128)S(1)} %get-tuple-element.27.base_ref, ...), custom_call_target="tpu_custom_call" | custom-call | flops 20000000 | bytes 6000000 | tf_op jit(solution)/shard_map/finish/pallas_call | solution.py:628
  (1 shorter events, 0.0 us)
Async XLA Ops:
  2.6 3.6 %collective-permute-start = (f32[40,128]{1,0:T(8,128)S(1)}, f32[40,128]{1,0:T(8,128)S(1)}, u32[]{:S(2)}, u32[]{:S(2)}) collective-permute-start(f32[40,128]{1,0:T(8,128)S(1)} %get-tuple-element.20), channel_id=1, source_target_pairs={{0,16},{4,20},{8,24},{12,28},{16,0},{20,4},{24,8},{28,12},{1,17},{... | collective-permute-start | bytes 61448 | tf_op jit(solution)/shard_map/ppermute | solution.py:571
  7.1 18.7 %copy-start = (f32[3,8,16,128]{3,2,1,0:T(8,128)S(1)}, f32[3,8,16,128]{3,2,1,0:T(8,128)}, u32[]{:S(2)}) copy-start(f32[3,8,16,128]{3,2,1,0:T(8,128)} %param.8) | copy-start | bytes 589828
  7.1 18.7 %copy-start.1 = (f32[3,8,16,128]{3,2,1,0:T(8,128)S(1)}, f32[3,8,16,128]{3,2,1,0:T(8,128)}, u32[]{:S(2)}) copy-start(f32[3,8,16,128]{3,2,1,0:T(8,128)} %param.9) | copy-start | bytes 589828
  7.1 18.7 %copy-start.2 = (f32[2,8,16,128]{3,2,1,0:T(8,128)S(1)}, f32[2,8,16,128]{3,2,1,0:T(8,128)}, u32[]{:S(2)}) copy-start(f32[2,8,16,128]{3,2,1,0:T(8,128)} %param.11) | copy-start | bytes 393220
  7.1 18.7 %copy-start.3 = (f32[8,16,128]{2,1,0:T(8,128)S(1)}, f32[8,16,128]{2,1,0:T(8,128)}, u32[]{:S(2)}) copy-start(f32[8,16,128]{2,1,0:T(8,128)} %param.10) | copy-start | bytes 196612
  7.1 30.4 %all-to-all-start = ((f32[16,80,128]{2,1,0:T(8,128)}), f32[16,80,128]{2,1,0:T(8,128)S(1)}, u32[]{:S(2)}, u32[]{:S(2)}) async-start(f32[16,80,128]{2,1,0:T(8,128)} %broadcast_in_dim.2), calls=%async_computation | async-start | bytes 1310720 | tf_op jit(solution)/shard_map/all_to_all | solution.py:575
  13.9 7.2 %collective-permute-start.1 = (f32[15,8,128]{2,1,0:T(8,128)S(1)}, f32[15,8,128]{2,1,0:T(8,128)S(1)}, u32[]{:S(2)}, u32[]{:S(2)}) collective-permute-start(f32[15,8,128]{2,1,0:T(8,128)S(1)} %get-tuple-element.21), channel_id=1, source_target_pairs={{0,4},{4,8},{8,12},{12,16},{16,20},{20,24},{24,28},{1,5},{5,9},{9,... | collective-permute-start | bytes 184328 | tf_op jit(solution)/shard_map/ppermute | solution.py:572
  17.1 8.6 %collective-permute-start.2 = (f32[15,8,128]{2,1,0:T(8,128)S(1)}, f32[15,8,128]{2,1,0:T(8,128)S(1)}, u32[]{:S(2)}, u32[]{:S(2)}) collective-permute-start(f32[15,8,128]{2,1,0:T(8,128)S(1)} %get-tuple-element.22.own_ref), channel_id=1, source_target_pairs={{4,0},{8,4},{12,8},{16,12},{20,16},{24,20},{28,24},{5,1},{9,5},{13... | collective-permute-start | bytes 184328 | tf_op jit(solution)/shard_map/ppermute | solution.py:573
  26.2 8.6 %collective-permute-start.3 = (f32[4,8,128]{2,1,0:T(8,128)S(1)}, f32[4,8,128]{2,1,0:T(8,128)S(1)}, u32[]{:S(2)}, u32[]{:S(2)}) collective-permute-start(f32[4,8,128]{2,1,0:T(8,128)S(1)} %get-tuple-element.23), channel_id=1, source_target_pairs={{0,1},{1,2},{2,3},{4,5},{5,6},{6,7},{8,9},{9,10},{10,11},{12,13},{... | collective-permute-start | bytes 49160 | tf_op jit(solution)/shard_map/ppermute | solution.py:592
  30.2 5.1 %collective-permute-start.4 = (f32[4,8,128]{2,1,0:T(8,128)S(1)}, f32[4,8,128]{2,1,0:T(8,128)S(1)}, u32[]{:S(2)}, u32[]{:S(2)}) collective-permute-start(f32[4,8,128]{2,1,0:T(8,128)S(1)} %get-tuple-element.24), channel_id=1, source_target_pairs={{1,0},{2,1},{3,2},{5,4},{6,5},{7,6},{9,8},{10,9},{11,10},{13,12},{... | collective-permute-start | bytes 49160 | tf_op jit(solution)/shard_map/ppermute | solution.py:593
  32.1 0.7 %copy-start.4 = (s32[64]{0:T(128)S(1)}, s32[64]{0:T(128)}, u32[]{:S(2)}) copy-start(s32[64]{0:T(128)} %route_ref.1) | copy-start | bytes 772

commit v4 on v3

--- a/solution.py
+++ b/solution.py
@@ -48,6 +48,11 @@
 
 def rows_loop(start, stop, most, body):
     step = max(d for d in range(1, most + 1) if (stop - start) % d == 0)
+
+    if step == stop - start:
+        for x in range(start, stop):
+            body(x)
+        return
 
     def chunk(i, carry):
         for r in range(step):
@@ -314,15 +319,15 @@
         for i in range(3):
             flow[i, x] = parts[i]
 
-    rows_loop(0, rows + 4, 10, first)
-    rows_loop(1, rows + 3, 6, lambda x: coef_row(mods_ref, coef, x))
+    rows_loop(0, rows + 4, rows + 4, first)
+    rows_loop(1, rows + 3, rows + 2, lambda x: coef_row(mods_ref, coef, x))
 
     def second(x):
         applied = apply_row(lambda c, r: now_x[c, r], lambda i, r: flow[i, r], coef, x, WIDE)
         for c in range(3):
             base_ref[c, x] = 2.0 * now_x[c, x] - base_ref[c, x] + scale_ref[x] * applied[c]
 
-    rows_loop(1, rows + 3, 9, second)
+    rows_loop(1, rows + 3, rows + 2, second)
 
     group_of_sub = sub // 2
     second_level = (sub - 2 * group_of_sub).astype(jnp.float32)
@@ -376,10 +381,12 @@
                 side_hat_ref[t, LANE:, :] = jnp.where(k_lane >= LANE // 2, hat, 0.0).astype(jnp.bfloat16)
 
 
-def split_dot(ref, hat):
-    v = ref[...]
+def split_dot(v, hat):
     high = v.astype(jnp.bfloat16)
     low = (v - high.astype(jnp.float32)).astype(jnp.bfloat16)
+    if v.shape[1] == LANE:
+        both = jnp.concatenate([high, low], axis=1)
+        return jnp.dot(both, jnp.concatenate([hat, hat], axis=0), preferred_element_type=jnp.float32)
     return jnp.dot(high, hat, preferred_element_type=jnp.float32) + jnp.dot(
         low, hat, preferred_element_type=jnp.float32
     )
@@ -388,13 +395,16 @@
 def finish_kernel(
     lev, rows, groups, c_east, c_north, got_ref, index_ref, mods_ref, base_ref, scale_ref, mask_ref,
     level_ref, shift_ref, own_hat_ref, side_hat_ref, now_ref, inc_out, mid_out, next_out,
-    mixed, own_rows, side_rows, north, parts, flow, mid, coef
+    mixed, own_rows, side_rows, north, parts, flow, mid, coef, inc_held, mid_held, next_held, sems
 ):
     lane = lane_ids((8, LANE))
-    rows_loop(0, rows + 4, 5, lambda x: quarter_row(mods_ref, coef, x))
-    rows_loop(1, rows + 3, 6, lambda x: coef_row(mods_ref, coef, x))
-
-    def tile_row(t, carry):
+    outs = ((inc_held, inc_out), (mid_held, mid_out), (next_held, next_out))
+    rows_loop(0, rows + 4, rows + 4, lambda x: quarter_row(mods_ref, coef, x))
+    rows_loop(1, rows + 3, rows + 2, lambda x: coef_row(mods_ref, coef, x))
+
+    def tile_row(t):
+        cells = range(rows) if t == 1 else range(rows - 2, rows) if t == 0 else range(2)
+        used = range(4 * cells[0] // 25, (4 * (cells[-1] + 24)) // 25 + 2)
         for column in range(3):
             pieces = []
             for g in range(groups):
@@ -411,7 +421,7 @@
                         (pltpu.roll(got_ref[source, 16:24, :], 4 * k, 0), pltpu.roll(tail, 4 * k, 0)),
                     )
                 )
-            for a in range(c_east):
+            for a in used:
                 start = a * c_north
                 for half in range(2):
                     total = jnp.zeros((8, LANE), jnp.float32)
@@ -429,29 +439,33 @@
                                 pltpu.roll(tail, (at - start) % LANE, 1),
                             )
                         total = jnp.where((lane >= at) & (lane < at + c_north), moved, total)
-                    mixed[a, 8 * half : 8 * half + 8, :] = total
+                    mixed[t, column, a, 8 * half : 8 * half + 8, :] = total
             w0 = level_ref[t, column, 0]
             w1 = level_ref[t, column, 1]
             for nc in range(6):
                 r = (nc // 3) * 6 + 2 * (nc % 3)
-                for a in range(c_east):
-                    value = w0 * jnp.broadcast_to(mixed[a, r : r + 1, :], (lev, LANE)) + w1 * jnp.broadcast_to(
-                        mixed[a, r + 1 : r + 2, :], (lev, LANE)
+                for a in used:
+                    value = w0 * jnp.broadcast_to(mixed[t, column, a, r : r + 1, :], (lev, LANE)) + w1 * jnp.broadcast_to(
+                        mixed[t, column, a, r + 1 : r + 2, :], (lev, LANE)
                     )
-                    at = (nc * c_east + a) * lev
+                    at = (nc * len(used) + a - used[0]) * lev
                     if column == 0:
-                        own_rows[at : at + lev, :] = value
+                        own_rows[t, at : at + lev, :] = value
                     elif column == 1:
-                        side_rows[at : at + lev, :LANE] = value
+                        side_rows[t, at : at + lev, :LANE] = value
                     else:
-                        side_rows[at : at + lev, LANE:] = value
-        own = split_dot(own_rows, own_hat_ref[t])
-        north[t, :, :, :LANE] = own.reshape(6 * c_east, lev, LANE)
-        side = split_dot(side_rows, side_hat_ref[t])
-        north[t, :, :, LANE:] = side.reshape(6 * c_east, lev, LANE)
-        return carry
-
-    lax.fori_loop(0, 3, tile_row, 0)
+                        side_rows[t, at : at + lev, LANE:] = value
+        count = 6 * len(used) * lev
+        own = split_dot(own_rows[t, :count, :], own_hat_ref[t])
+        side = split_dot(side_rows[t, :count, :], side_hat_ref[t])
+        for nc in range(6):
+            part = slice(nc * len(used) * lev, (nc + 1) * len(used) * lev)
+            to = slice(nc * c_east + used[0], nc * c_east + used[-1] + 1)
+            north[t, to, :, :LANE] = own[part].reshape(len(used), lev, LANE)
+            north[t, to, :, LANE:] = side[part].reshape(len(used), lev, LANE)
+
+    for t in range(3):
+        tile_row(t)
 
     near = (4 * 24) // 25 + 3
 
@@ -471,18 +485,20 @@
             values.append(total)
             parts[nc, x] = outer * total
             parts[6 + nc, x] = inner * total
-            if not isinstance(cell, int):
-                inc_out[pl.ds(nc * lev * rows + cell, lev, stride=rows), :] = total[:, :LANE]
+            if t == 1:
+                inc_held[pl.ds(nc * lev * rows + cell, lev, stride=rows), :] = total[:, :LANE]
         for n in range(2):
             for q, mask in enumerate((outer, inner)):
                 moved = east_flow([mask * values[3 * n + c] for c in range(3)], coef, x)
                 for i in range(3):
                     flow[6 * n + 3 * q + i, x] = moved[i]
 
-    rows_loop(0, rows, 8, lambda cell: east(cell + 2, 1, cell))
+    rows_loop(0, rows, rows, lambda cell: east(cell + 2, 1, cell))
     for r in range(2):
         east(r, 0, rows - 2 + r)
         east(rows + 2 + r, 2, r)
+    sends = [pltpu.make_async_copy(a, b, sems.at[i]) for i, (a, b) in enumerate(outs)]
+    sends[0].start()
 
     def forcing(step, x, t, width):
         outside = apply_row(
@@ -495,20 +511,25 @@
         inner = mask_ref[1, t][:, :width]
         return [inner * outside[c] - outer * inside[c] for c in range(3)]
 
-    def middle(x):
-        t = (x >= 2).astype(jnp.int32) + (x >= rows + 2).astype(jnp.int32)
+    def middle(x, t):
         force = forcing(0, x, t, WIDE)
         for c in range(3):
-            mid[c, x] = base_ref[c, x] + scale_ref[x] * force[c]
-
-    rows_loop(1, rows + 3, 9, middle)
+            value = base_ref[c, x] + scale_ref[x] * force[c]
+            mid[c, x] = value
+            if t == 1:
+                mid_held[pl.ds(c * lev * rows + x - 2, lev, stride=rows), :] = value[:, :LANE]
+
+    middle(1, 0)
+    rows_loop(2, rows + 2, rows // 2, lambda x: middle(x, 1))
+    middle(rows + 2, 2)
+    sends[1].start()
 
     def flows(x):
         moved = east_flow([mid[c, x] for c in range(3)], coef, x)
         for i in range(3):
             flow[12 + i, x] = moved[i]
 
-    rows_loop(1, rows + 3, 18, flows)
+    rows_loop(1, rows + 3, rows + 2, flows)
 
     def last(x):
         force = forcing(1, x, 1, LANE)
@@ -517,12 +538,14 @@
         for c in range(3):
             now = now_ref[pl.ds(c * lev * rows + x - 2, lev, stride=rows), :]
             current = mid[c, x, :, :LANE]
-            mid_out[pl.ds(c * lev * rows + x - 2, lev, stride=rows), :] = current
-            next_out[pl.ds(c * lev * rows + x - 2, lev, stride=rows), :] = (
+            next_held[pl.ds(c * lev * rows + x - 2, lev, stride=rows), :] = (
                 2.0 * current - now + scale * (applied[c] + force[c])
             )
 
-    rows_loop(2, rows + 2, 16, last)
+    rows_loop(2, rows + 2, rows, last)
+    sends[2].start()
+    for send in sends:
+        send.wait()
 
 
 def specs(text):
@@ -633,16 +656,20 @@
             f32(3 * lev * rows, LANE),
         ),
         in_specs=specs("vsvvvvvvvvv"),
-        out_specs=specs("vvv"),
+        out_specs=specs("hhh"),
         scratch_shapes=[
-            VMEM((c_east, 16, LANE), jnp.float32),
-            VMEM((6 * c_east * lev, LANE), jnp.float32),
-            VMEM((6 * c_east * lev, WIDE), jnp.float32),
+            VMEM((3, 3, c_east, 16, LANE), jnp.float32),
+            VMEM((3, 6 * c_east * lev, LANE), jnp.float32),
+            VMEM((3, 6 * c_east * lev, WIDE), jnp.float32),
             VMEM((3, 6 * c_east, lev, WIDE), jnp.float32),
             VMEM((12, wide, lev, WIDE), jnp.float32),
             VMEM((15, wide, lev, WIDE), jnp.float32),
             VMEM((3, wide, lev, WIDE), jnp.float32),
             VMEM((COEFS, wide, lev, WIDE), jnp.float32),
+            VMEM((6 * lev * rows, LANE), jnp.float32),
+            VMEM((3 * lev * rows, LANE), jnp.float32),
+            VMEM((3 * lev * rows, LANE), jnp.float32),
+            pltpu.SemaphoreType.DMA((3,)),
         ],
         cost_estimate=pl.CostEstimate(flops=20000000, bytes_accessed=6000000, transcendentals=0),
         compiler_params=limit,

time: 45 us -> 43.4 us (0.964)
  Pallas kernels: 13.8 us -> 12.2 us
    pallas_call x1, Pallas kernels: 7.16 us -> 6.11 us  [local(): pl.pallas_call(functools.partial(finish_kernel, lev, rows, groups, c_east...]
    pallas_call x1, Pallas kernels: 2.2 us -> 1.66 us  [local(): pl.pallas_call(functools.partial(prep_kernel, lev, rows, groups, c_north)...]
where the time goes in v4:
time: 43.4 us; the launch traced here: 43 us
  starting transfers between devices  18.9 us (44%)
  Pallas kernels  12.2 us (28%)
  waiting for transfers between devices  9.65 us (22%)
  local copies, waits for them, and re-layouts  1.48 us (3%)
  between operations  0.75 us (2%)
    all_to_all x1, starting transfers between devices, local(): lax.all_to_all(jnp.broadcast_to(chunk[None], (half,) + chunk.shape), ('gx...  6.82 us
    pallas_call x1, Pallas kernels, local(): pl.pallas_call(functools.partial(finish_kernel, lev, rows, groups, c_east...  6.11 us
    ppermute x1, waiting for transfers between devices, local(): after = lax.ppermute(first, 'gx', neighbours('gx', -1))  4.7 us
    ppermute x1, starting transfers between devices, local(): west = lax.ppermute(to_east, 'gy', neighbours('gy', 1))  3.95 us
    ppermute x1, waiting for transfers between devices, local(): lax.ppermute(payload, 'gx', [(i, (i + n_x // 2) % n_x) for i in range(n_x)])  3.52 us
    ppermute x1, starting transfers between devices, local(): before = lax.ppermute(last, 'gx', neighbours('gx', 1))  3.25 us
    ppermute x1, starting transfers between devices, local(): after = lax.ppermute(first, 'gx', neighbours('gx', -1))  2.92 us
    pallas_call x1, Pallas kernels, local(): pl.pallas_call(functools.partial(index_kernel, groups, n_x, n_y), out_sha...  2.02 us
  transfers between devices with their start and end apart: 6, of which 4 were waited for; matrix products, arithmetic and copies ran while one was open for 0% of the time, Pallas kernels for 10%

profile of v4, /device:TPU:17, one launch (start us, length us, event | category | flops | bytes accessed | tf_op | source)
XLA Modules:
  0.0 43.0 jit_solution(5253137056547645318)
XLA Ops:
  0.6 1.9 %pre.1 = (f32[40,128]{1,0:T(8,128)S(1)}, f32[15,8,128]{2,1,0:T(8,128)S(1)}, f32[15,8,128]{2,1,0:T(8,128)S(1)}) custom-call(f32[2,24,256]{2,1,0:T(8,128)} %refs_0_.1, f32[384,128]{1,0:T(8,128)} %bitcast.11, f32[384,128]{1,0:T(8,128)} %bitcast.16, f32[128,128]{1,0:T(8,128)} %bitcast.22, f32[256,128]{1,0:T(8,128)} %bitcast.19, s32[1,3,1,4]{3,2,1,0:T(1,128)} %bitcast.25, ...), custom_call_target="tpu_custom_call" | custom-call | tf_op jit(solution)/shard_map/pre/pallas_call | solution.py:582
  2.6 0.1 collective-permute-start
  2.6 3.5 %collective-permute-done = f32[40,128]{1,0:T(8,128)S(1)} collective-permute-done((f32[40,128]{1,0:T(8,128)S(1)}, f32[40,128]{1,0:T(8,128)S(1)}, u32[]{:S(2)}, u32[]{:S(2)}) %collective-permute-start) | collective-permute-done | bytes 20512 | tf_op jit(solution)/shard_map/ppermute | solution.py:594
  6.2 0.9 %broadcast_in_dim.2 = f32[16,80,128]{2,1,0:T(8,128)} broadcast(f32[80,128]{1,0:T(8,128)S(1)} %pad_maximum_fusion), dimensions={1,2} | broadcast | bytes 696320 | tf_op jit(solution)/shard_map/broadcast_in_dim | solution.py:599
  7.1 0.0 copy-start
  7.1 0.0 copy-start.1
  7.1 0.0 copy-start.2
  7.1 0.0 copy-start.3
  7.1 6.8 %all-to-all-start = ((f32[16,80,128]{2,1,0:T(8,128)}), f32[16,80,128]{2,1,0:T(8,128)S(1)}, u32[]{:S(2)}, u32[]{:S(2)}) async-start(f32[16,80,128]{2,1,0:T(8,128)} %broadcast_in_dim.2), calls=%async_computation | async-start | bytes 1310720 | tf_op jit(solution)/shard_map/all_to_all | solution.py:598
  13.9 3.2 %collective-permute-start.1 = (f32[15,8,128]{2,1,0:T(8,128)S(1)}, f32[15,8,128]{2,1,0:T(8,128)S(1)}, u32[]{:S(2)}, u32[]{:S(2)}) collective-permute-start(f32[15,8,128]{2,1,0:T(8,128)S(1)} %get-tuple-element.21), channel_id=1, source_target_pairs={{0,4},{4,8},{8,12},{12,16},{16,20},{20,24},{24,28},{1,5},{5,9},{9,... | collective-permute-start | bytes 184328 | tf_op jit(solution)/shard_map/ppermute | solution.py:595
  17.1 2.9 %collective-permute-start.2 = (f32[15,8,128]{2,1,0:T(8,128)S(1)}, f32[15,8,128]{2,1,0:T(8,128)S(1)}, u32[]{:S(2)}, u32[]{:S(2)}) collective-permute-start(f32[15,8,128]{2,1,0:T(8,128)S(1)} %get-tuple-element.22.own_ref), channel_id=1, source_target_pairs={{4,0},{8,4},{12,8},{16,12},{20,16},{24,20},{28,24},{5,1},{9,5},{13... | collective-permute-start | bytes 184328 | tf_op jit(solution)/shard_map/ppermute | solution.py:596
  20.1 1.0 %collective-permute-done.1.before_ref = f32[15,8,128]{2,1,0:T(8,128)S(1)} collective-permute-done((f32[15,8,128]{2,1,0:T(8,128)S(1)}, f32[15,8,128]{2,1,0:T(8,128)S(1)}, u32[]{:S(2)}, u32[]{:S(2)}) %collective-permute-start.1) | collective-permute-done | bytes 61472 | tf_op jit(solution)/shard_map/ppermute | solution.py:595
  21.1 4.7 %collective-permute-done.2.after_ref = f32[15,8,128]{2,1,0:T(8,128)S(1)} collective-permute-done((f32[15,8,128]{2,1,0:T(8,128)S(1)}, f32[15,8,128]{2,1,0:T(8,128)S(1)}, u32[]{:S(2)}, u32[]{:S(2)}) %collective-permute-start.2) | collective-permute-done | bytes 61472 | tf_op jit(solution)/shard_map/ppermute | solution.py:596
  25.8 0.0 copy-done
  25.8 0.0 copy-done.1
  25.8 0.0 copy-done.2
  25.8 0.0 copy-done.3
  25.8 0.4 %pack.1 = (f32[4,8,128]{2,1,0:T(8,128)S(1)}, f32[4,8,128]{2,1,0:T(8,128)S(1)}, f32[8,128]{1,0:T(8,128)S(1)}) custom-call(f32[384,128]{1,0:T(8,128)S(1)} %bitcast.12, f32[384,128]{1,0:T(8,128)S(1)} %bitcast.17, f32[128,128]{1,0:T(8,128)S(1)} %bitcast.23, f32[256,128]{1,0:T(8,128)S(1)} %bitcast.20, f32[15,8,128]{2,1,0:T(8,128)S(1)} %collective-permute-done.1.before_ref, ...), custom_call_target="tpu_custom_call" | custom-call | flops 2000000 | bytes 1000000 | tf_op jit(solution)/shard_map/pack/pallas_call | solution.py:606
  26.2 3.9 %collective-permute-start.3 = (f32[4,8,128]{2,1,0:T(8,128)S(1)}, f32[4,8,128]{2,1,0:T(8,128)S(1)}, u32[]{:S(2)}, u32[]{:S(2)}) collective-permute-start(f32[4,8,128]{2,1,0:T(8,128)S(1)} %get-tuple-element.23), channel_id=1, source_target_pairs={{0,1},{1,2},{2,3},{4,5},{5,6},{6,7},{8,9},{9,10},{10,11},{12,13},{... | collective-permute-start | bytes 49160 | tf_op jit(solution)/shard_map/ppermute | solution.py:615
  30.2 1.9 %collective-permute-start.4 = (f32[4,8,128]{2,1,0:T(8,128)S(1)}, f32[4,8,128]{2,1,0:T(8,128)S(1)}, u32[]{:S(2)}, u32[]{:S(2)}) collective-permute-start(f32[4,8,128]{2,1,0:T(8,128)S(1)} %get-tuple-element.24), channel_id=1, source_target_pairs={{1,0},{2,1},{3,2},{5,4},{6,5},{7,6},{9,8},{10,9},{11,10},{13,12},{... | collective-permute-start | bytes 49160 | tf_op jit(solution)/shard_map/ppermute | solution.py:616
  32.1 0.0 copy-start.4
  32.1 0.1 pad_add_fusion.place_ref
  32.2 0.6 %copy-done.4 = s32[64]{0:T(128)S(1)} copy-done((s32[64]{0:T(128)S(1)}, s32[64]{0:T(128)}, u32[]{:S(2)}) %copy-start.4) | copy-done | bytes 280
  32.8 2.0 %index.1.index_ref = s32[37]{0:T(128)S(1)} custom-call(s32[64]{0:T(128)S(1)} %copy-done.4, s32[2]{0:T(128)S(1)} %pad_add_fusion.place_ref), custom_call_target="tpu_custom_call" | custom-call | flops 2000000 | bytes 1000 | tf_op jit(solution)/shard_map/index/pallas_call | solution.py:618
  34.8 0.0 collective-permute-done.3.west_ref
  34.8 0.4 %collective-permute-done.4.east_ref = f32[4,8,128]{2,1,0:T(8,128)S(1)} collective-permute-done((f32[4,8,128]{2,1,0:T(8,128)S(1)}, f32[4,8,128]{2,1,0:T(8,128)S(1)}, u32[]{:S(2)}, u32[]{:S(2)}) %collective-permute-start.4) | collective-permute-done | bytes 16416 | tf_op jit(solution)/shard_map/ppermute | solution.py:616
  35.3 1.7 %prep.1 = (f32[2,20,8,256]{3,2,1,0:T(8,128)S(1)}, f32[3,20,8,256]{3,2,1,0:T(8,128)S(1)}, f32[20,8,256]{2,1,0:T(8,128)S(1)}, f32[2,3,8,256]{3,2,1,0:T(8,128)S(1)}...) custom-call(f32[384,128]{1,0:T(8,128)S(1)} %bitcast.13, ...), custom_call_target="tpu_custom_call" | custom-call | flops 10000000 | bytes 3000000 | tf_op jit(solution)/shard_map/prep/pallas_call | solution.py:627
  36.9 0.0 all-to-all-done
  36.9 6.1 %finish.1 = (f32[768,128]{1,0:T(8,128)}, f32[384,128]{1,0:T(8,128)}, f32[384,128]{1,0:T(8,128)}) custom-call(f32[32,40,128]{2,1,0:T(8,128)S(1)} %bitcast.15, s32[37]{0:T(128)S(1)} %index.1.index_ref, f32[2,20,8,256]{3,2,1,0:T(8,128)S(1)} %get-tuple-element.26.mods_ref, f32[3,20,8,256]{3,2,1,0:T(8,128)S(1)} %get-tuple-element.27.base_ref, ...), custom_call_target="tpu_custom_call" | custom-call | flops 20000000 | bytes 6000000 | tf_op jit(solution)/shard_map/finish/pallas_call | solution.py:651
  (1 shorter events, 0.0 us)
Async XLA Ops:
  2.6 3.6 %collective-permute-start = (f32[40,128]{1,0:T(8,128)S(1)}, f32[40,128]{1,0:T(8,128)S(1)}, u32[]{:S(2)}, u32[]{:S(2)}) collective-permute-start(f32[40,128]{1,0:T(8,128)S(1)} %get-tuple-element.20), channel_id=1, source_target_pairs={{0,16},{4,20},{8,24},{12,28},{16,0},{20,4},{24,8},{28,12},{1,17},{... | collective-permute-start | bytes 61448 | tf_op jit(solution)/shard_map/ppermute | solution.py:594
  7.1 18.7 %copy-start = (f32[3,8,16,128]{3,2,1,0:T(8,128)S(1)}, f32[3,8,16,128]{3,2,1,0:T(8,128)}, u32[]{:S(2)}) copy-start(f32[3,8,16,128]{3,2,1,0:T(8,128)} %param.8) | copy-start | bytes 589828
  7.1 18.7 %copy-start.1 = (f32[3,8,16,128]{3,2,1,0:T(8,128)S(1)}, f32[3,8,16,128]{3,2,1,0:T(8,128)}, u32[]{:S(2)}) copy-start(f32[3,8,16,128]{3,2,1,0:T(8,128)} %param.9) | copy-start | bytes 589828
  7.1 18.7 %copy-start.2 = (f32[2,8,16,128]{3,2,1,0:T(8,128)S(1)}, f32[2,8,16,128]{3,2,1,0:T(8,128)}, u32[]{:S(2)}) copy-start(f32[2,8,16,128]{3,2,1,0:T(8,128)} %param.11) | copy-start | bytes 393220
  7.1 18.7 %copy-start.3 = (f32[8,16,128]{2,1,0:T(8,128)S(1)}, f32[8,16,128]{2,1,0:T(8,128)}, u32[]{:S(2)}) copy-start(f32[8,16,128]{2,1,0:T(8,128)} %param.10) | copy-start | bytes 196612
  7.1 29.9 %all-to-all-start = ((f32[16,80,128]{2,1,0:T(8,128)}), f32[16,80,128]{2,1,0:T(8,128)S(1)}, u32[]{:S(2)}, u32[]{:S(2)}) async-start(f32[16,80,128]{2,1,0:T(8,128)} %broadcast_in_dim.2), calls=%async_computation | async-start | bytes 1310720 | tf_op jit(solution)/shard_map/all_to_all | solution.py:598
  13.9 7.2 %collective-permute-start.1 = (f32[15,8,128]{2,1,0:T(8,128)S(1)}, f32[15,8,128]{2,1,0:T(8,128)S(1)}, u32[]{:S(2)}, u32[]{:S(2)}) collective-permute-start(f32[15,8,128]{2,1,0:T(8,128)S(1)} %get-tuple-element.21), channel_id=1, source_target_pairs={{0,4},{4,8},{8,12},{12,16},{16,20},{20,24},{24,28},{1,5},{5,9},{9,... | collective-permute-start | bytes 184328 | tf_op jit(solution)/shard_map/ppermute | solution.py:595
  17.1 8.6 %collective-permute-start.2 = (f32[15,8,128]{2,1,0:T(8,128)S(1)}, f32[15,8,128]{2,1,0:T(8,128)S(1)}, u32[]{:S(2)}, u32[]{:S(2)}) collective-permute-start(f32[15,8,128]{2,1,0:T(8,128)S(1)} %get-tuple-element.22.own_ref), channel_id=1, source_target_pairs={{4,0},{8,4},{12,8},{16,12},{20,16},{24,20},{28,24},{5,1},{9,5},{13... | collective-permute-start | bytes 184328 | tf_op jit(solution)/shard_map/ppermute | solution.py:596
  26.2 8.6 %collective-permute-start.3 = (f32[4,8,128]{2,1,0:T(8,128)S(1)}, f32[4,8,128]{2,1,0:T(8,128)S(1)}, u32[]{:S(2)}, u32[]{:S(2)}) collective-permute-start(f32[4,8,128]{2,1,0:T(8,128)S(1)} %get-tuple-element.23), channel_id=1, source_target_pairs={{0,1},{1,2},{2,3},{4,5},{5,6},{6,7},{8,9},{9,10},{10,11},{12,13},{... | collective-permute-start | bytes 49160 | tf_op jit(solution)/shard_map/ppermute | solution.py:615
  30.2 5.1 %collective-permute-start.4 = (f32[4,8,128]{2,1,0:T(8,128)S(1)}, f32[4,8,128]{2,1,0:T(8,128)S(1)}, u32[]{:S(2)}, u32[]{:S(2)}) collective-permute-start(f32[4,8,128]{2,1,0:T(8,128)S(1)} %get-tuple-element.24), channel_id=1, source_target_pairs={{1,0},{2,1},{3,2},{5,4},{6,5},{7,6},{9,8},{10,9},{11,10},{13,12},{... | collective-permute-start | bytes 49160 | tf_op jit(solution)/shard_map/ppermute | solution.py:616
  32.1 0.7 %copy-start.4 = (s32[64]{0:T(128)S(1)}, s32[64]{0:T(128)}, u32[]{:S(2)}) copy-start(s32[64]{0:T(128)} %route_ref.1) | copy-start | bytes 772
